TPU v7x, 128 devices: a whole 4x4x4 slice. The times are simulated.
128 devices in a mesh: seq: 16 (over y, x), batch: 8 (over z, core).
Axes of the slice: x: 4, y: 4, z: 4, core: 2. Of those that a mesh axis runs over, the one named last changes fastest.
Arguments:
- queries: bfloat16 [16384, 4096], P(('batch', 'seq')), parts along dimension 0, may hold values from -6 to 6
- key_vectors: bfloat16 [16384, 4096], P(('batch', 'seq')), parts along dimension 0, may hold values from -6 to 6
- value_vectors: bfloat16 [16384, 4096], P(('batch', 'seq')), parts along dimension 0, may hold values from -6 to 6
- residual_in: bfloat16 [16384, 4096], P(('batch', 'seq')), parts along dimension 0, may hold values from -6 to 6
- input_logit: float32 [8, 16384], P(None, ('batch', 'seq')), parts along dimension 1, may hold values from -8 to 300
- forget_logit: float32 [8, 16384], P(None, ('batch', 'seq')), parts along dimension 1, may hold values from -3 to 13
- mix_gain: float32 [4096], replicated, may hold values from 0.1 to 1.9
- ffn_gain: float32 [4096], replicated, may hold values from 0.1 to 1.9
- expert_gate: bfloat16 [16, 4096, 704], P('seq'), may hold values from -0.09375 to 0.09375
- expert_up: bfloat16 [16, 4096, 704], P('seq'), may hold values from -0.09375 to 0.09375
- expert_down: bfloat16 [16, 704, 4096], P('seq'), may hold values from -0.21875 to 0.21875
- routes: int32 [16384, 2], P(('batch', 'seq')), parts along dimension 0, may hold values from 0 to 15, all different within a row; in each aligned block of 128 rows (0 to 127, 128 to 255, ...) at most 32 rows name the same one
- route_weight: float32 [16384, 2], P(('batch', 'seq')), parts along dimension 0, may hold values from 0.2 to 1
Outputs:
- block_out: bfloat16 [16384, 4096], P(('batch', 'seq')), parts along dimension 0
There are 8 independent parts, one for each index of `batch`. A program takes and returns all parts, laid end to end along the dimension named above; an argument that names none is the same for every part. Nothing has to cross between parts.
Inputs may be any that keep to these rules, and one draw needn't show every extreme that they name: `routes`: each row names two different experts. Within the rows of one device no expert is named by more than 32 rows, and in some device one expert is named by exactly 32 rows.
All inputs are finite; a program needn't handle non-finite values.
Results may differ from a plain program's by a relative error of at most 0.0081.
Values may be sent and summed in bfloat16 or wider, within the bound.
A program may use at most 128 MiB of HBM per device.

v0:
```python
import math

import jax
import jax.numpy as jnp
from jax import lax
from jax.sharding import PartitionSpec as P

NEG_FILL = -1e30
EPSILON = 1e-06


def in_one_piece(arrays, axis, split_dim, concat_dim, along):
    widths = [a.shape[along] for a in arrays]
    both = jnp.concatenate(arrays, axis=along)
    out = lax.all_to_all(both, axis, split_axis=split_dim, concat_axis=concat_dim, tiled=True)
    return tuple(jnp.split(out, [sum(widths[:k]) for k in range(1, len(widths))], axis=along))


def side_by_side(arrays, axis, dim, along):
    both = jnp.concatenate(arrays, axis=along)
    out, at, gathered = (lax.all_gather(both, axis, axis=dim, tiled=True), 0, [])
    for a in arrays:
        gathered.append(lax.slice_in_dim(out, at, at + a.shape[along], axis=along))
        at += a.shape[along]
    return tuple(gathered)


def items_in_groups(shard, axis, split_dim, concat_dim, work, item_dim, out_dim):
    items = jax.tree.leaves(shard)[0].shape[item_dim]
    count = 2 if items % 2 == 0 else 1
    gathered = []
    for k in range(count):
        group = jax.tree.map(
            lambda a: lax.slice_in_dim(
                a, k * (items // count), (k + 1) * (items // count), axis=item_dim
            ),
            shard,
        )
        gathered.append(
            work(
                lax.all_to_all(
                    group, axis, split_axis=split_dim, concat_axis=concat_dim, tiled=True
                )
            )
        )
    return jax.tree.map(lambda *parts: jnp.concatenate(parts, axis=out_dim), *gathered)


def join_states(earlier, later):
    total_early, state_early, normv_early, peak_early = earlier
    total_late, state_late, normv_late, peak_late = later
    carried = total_late + peak_early
    peak_new = jnp.maximum(carried, peak_late)
    scale_early = jnp.exp(carried - peak_new)
    scale_late = jnp.exp(peak_late - peak_new)
    state_new = scale_early[..., None] * state_early + scale_late[..., None] * state_late
    normv_new = scale_early * normv_early + scale_late * normv_late
    return (total_early + total_late, state_new, normv_new, peak_new)


def block_state(keys_three, values_three, log_forget, input_gate):
    cumul_log = jnp.cumsum(log_forget, axis=1)
    tail_log = cumul_log[:, -1:] - cumul_log + input_gate
    peak_tail = jnp.max(tail_log, axis=1)
    weight = jnp.exp(tail_log - peak_tail[:, None])
    weighted = keys_three.astype(jnp.float32) * jnp.transpose(weight)[:, :, None]
    rounded = weighted.astype(jnp.bfloat16)
    state_mat = jnp.einsum(
        "thd,the->hde", rounded, values_three, preferred_element_type=jnp.float32
    )
    norm_vec = jnp.sum(weighted, axis=0)
    return (
        jnp.broadcast_to(cumul_log[:, -1:], norm_vec.shape),
        state_mat,
        norm_vec,
        jnp.broadcast_to(peak_tail[:, None], norm_vec.shape),
    )


def block_mix(queries_three, keys_three, values_three, log_forget, input_gate, carry_in):
    tokens = queries_three.shape[0]
    inverse_root = 1.0 / math.sqrt(queries_three.shape[2])
    cumul_log = jnp.cumsum(log_forget, axis=1)
    carry_total, carry_state, carry_norm, carry_peak = carry_in
    log_weight = cumul_log[:, :, None] - cumul_log[:, None, :] + input_gate[:, None, :]
    causal = jnp.arange(tokens)[:, None] >= jnp.arange(tokens)[None, :]
    log_weight = jnp.where(causal[None], log_weight, NEG_FILL)
    carried = cumul_log + carry_peak[:, 0:1]
    peak_log = jnp.maximum(jnp.max(log_weight, axis=2), carried)
    decay_mat = jnp.exp(log_weight - peak_log[:, :, None])
    scores = (
        jnp.einsum("thd,shd->hts", queries_three, keys_three, preferred_element_type=jnp.float32)
        * inverse_root
    )
    coef = decay_mat * scores
    denom_sum = jnp.sum(coef, axis=2)
    numer_sum = jnp.einsum(
        "hts,she->the", coef.astype(jnp.bfloat16), values_three, preferred_element_type=jnp.float32
    )
    carry_reach = jnp.exp(carried - peak_log) * inverse_root
    query_float = queries_three.astype(jnp.float32)
    from_state = jnp.einsum(
        "thd,hde->the", query_float, carry_state, precision=lax.Precision.HIGHEST
    )
    from_norm = jnp.einsum("thd,hd->ht", query_float, carry_norm, precision=lax.Precision.HIGHEST)
    numer_sum = numer_sum + jnp.transpose(carry_reach)[:, :, None] * from_state
    denom_sum = denom_sum + carry_reach * from_norm
    floor_sum = jnp.maximum(jnp.abs(denom_sum), 1.0)
    return numer_sum / jnp.transpose(floor_sum)[:, :, None]


def shards(
    queries,
    key_vectors,
    value_vectors,
    residual_in,
    input_logit,
    forget_logit,
    mix_gain,
    ffn_gain,
    expert_gate,
    expert_up,
    expert_down,
    routes,
    route_weight,
):
    tokens, model_width = queries.shape
    head_count = input_logit.shape[0]
    head_dim = model_width // head_count
    devices = lax.axis_size("seq")
    queries_three = queries.reshape(tokens, head_count, head_dim)
    keys_three = key_vectors.reshape(tokens, head_count, head_dim)
    group = devices // head_count
    group_width = model_width // devices
    query_send = jnp.repeat(queries_three, group, axis=1)
    key_send = jnp.repeat(keys_three, group, axis=1)
    value_send = value_vectors.reshape(tokens, devices, group_width)
    query_all, key_all, value_all = in_one_piece((query_send, key_send, value_send), "seq", 1, 0, 2)
    input_all, forget_all = side_by_side((input_logit, forget_logit), "seq", 1, 0)
    head_index = lax.axis_index("seq") // group
    input_head = lax.dynamic_slice_in_dim(input_all, head_index, 1, 0)
    forget_head = jax.nn.log_sigmoid(lax.dynamic_slice_in_dim(forget_all, head_index, 1, 0))

    def per_block(array):
        return array.reshape((devices, tokens) + array.shape[1:])

    def per_gate(array):
        return jnp.transpose(array.reshape(1, devices, tokens), (1, 0, 2))

    start = (
        jnp.zeros((1, head_dim), jnp.float32),
        jnp.zeros((1, head_dim, group_width), jnp.float32),
        jnp.zeros((1, head_dim), jnp.float32),
        jnp.full((1, head_dim), NEG_FILL, jnp.float32),
    )

    def advance(carry_in, pieces):
        query_block, key_block, value_block, forget_block, input_block = pieces
        result = block_mix(query_block, key_block, value_block, forget_block, input_block, carry_in)
        carry_out = join_states(
            carry_in, block_state(key_block, value_block, forget_block, input_block)
        )
        return (carry_out, result)

    unused, mixed = lax.scan(
        advance,
        start,
        (
            per_block(query_all),
            per_block(key_all),
            per_block(value_all),
            per_gate(forget_head),
            per_gate(input_head),
        ),
    )
    mixed = mixed.reshape(devices * tokens, 1, group_width)
    mixer_out = (
        lax.all_to_all(mixed.astype(jnp.bfloat16), "seq", split_axis=0, concat_axis=1, tiled=True)
        .astype(mixed.dtype)
        .reshape(tokens, model_width)
    )
    mixer_square = jnp.mean(mixer_out * mixer_out, axis=1, keepdims=True)
    updated = (
        residual_in.astype(jnp.float32) + mixer_out * lax.rsqrt(mixer_square + EPSILON) * mix_gain
    ).astype(jnp.bfloat16)
    updated_float = updated.astype(jnp.float32)
    updated_square = jnp.mean(updated_float * updated_float, axis=1, keepdims=True)
    normed = (updated_float * lax.rsqrt(updated_square + EPSILON) * ffn_gain).astype(jnp.bfloat16)
    capacity = 4 * tokens // devices
    flat_routes = routes.reshape(-1)
    matches = (flat_routes[:, None] == jnp.arange(devices, dtype=jnp.int32)[None, :]).astype(
        jnp.int32
    )
    before = jnp.cumsum(matches, axis=0) - matches
    position = jnp.sum(before * matches, axis=1)
    slot_index = (flat_routes * capacity + position).reshape(tokens, 2)
    columns = jnp.arange(devices * capacity, dtype=jnp.int32)
    pick_first = (slot_index[:, 0:1] == columns[None, :]).astype(jnp.bfloat16)
    pick_second = (slot_index[:, 1:2] == columns[None, :]).astype(jnp.bfloat16)
    spread = jnp.einsum(
        "tc,td->cd", pick_first + pick_second, normed, preferred_element_type=jnp.float32
    ).astype(jnp.bfloat16)
    outbound = spread.reshape(devices, capacity, model_width)

    def run_expert(block_in):
        row_block = block_in.reshape(-1, model_width)
        gate_val = jnp.dot(row_block, expert_gate[0], preferred_element_type=jnp.float32)
        up_val = jnp.dot(row_block, expert_up[0], preferred_element_type=jnp.float32)
        hidden = (jax.nn.silu(gate_val) * up_val).astype(jnp.bfloat16)
        result = jnp.dot(hidden, expert_down[0], preferred_element_type=jnp.float32).astype(
            jnp.bfloat16
        )
        return lax.all_to_all(
            result.reshape(block_in.shape), "seq", split_axis=0, concat_axis=0, tiled=True
        )

    inbound = items_in_groups(outbound, "seq", 0, 0, run_expert, 1, 1)
    flat_back = inbound.reshape(devices * capacity, model_width)
    first_out = jnp.dot(pick_first, flat_back, preferred_element_type=jnp.float32)
    second_out = jnp.dot(pick_second, flat_back, preferred_element_type=jnp.float32)
    expert_mix = route_weight[:, 0:1] * first_out + route_weight[:, 1:2] * second_out
    return (updated_float + expert_mix).astype(jnp.bfloat16)


def solution(mesh):
    return jax.shard_map(
        shards,
        mesh=mesh,
        in_specs=(
            P(("batch", "seq"), None),
            P(("batch", "seq"), None),
            P(("batch", "seq"), None),
            P(("batch", "seq"), None),
            P(None, ("batch", "seq")),
            P(None, ("batch", "seq")),
            P(),
            P(),
            P("seq", None, None),
            P("seq", None, None),
            P("seq", None, None),
            P(("batch", "seq"), None),
            P(("batch", "seq"), None),
        ),
        out_specs=P(("batch", "seq"), None),
        check_vma=False,
    )
```

profile of v0, /device:TPU:0, one launch (start us, length us, event | category | flops | bytes accessed | tf_op | source)
XLA Modules:
  0.0 463.0 jit_solution(2480184343876847461)
XLA Ops:
  0.0 1.5 copy.114
  2.4 2.8 pad_maximum_fusion
  5.2 7.3 %all-to-all-start = ((bf16[128,16,1280]{2,0,1:T(8,128)(2,1)}), bf16[128,16,1280]{2,0,1:T(8,128)(2,1)}, u32[]{:S(2)}, u32[]{:S(2)}) async-start(bf16[128,16,1280]{2,0,1:T(8,128)(2,1)} %pad_maximum_fusion), calls=%async_computation | async-start | bytes 10485760 | tf_op jit(solution)/shard_map/all_to_all | solution.py:15
  12.6 91.4 %all_gather.3 = f32[16,2048]{1,0:T(8,128)S(1)} all-gather(f32[16,128]{1,0:T(8,128)S(1)} %pad_maximum_fusion.2), channel_id=1, replica_groups=mesh['seq'=16,'batch'=8] {'seq'}, dimensions={1}, use_global_device_ids=true | all-gather | bytes 139264 | tf_op jit(solution)/shard_map/all_gather | solution.py:21
  104.1 3.9 fusion.111
  108.0 2.3 split.13
  110.3 202.9 %while.17 = (s32[]{:T(128)}, f32[1,512,256]{2,1,0:T(8,128)S(1)}, f32[1,512]{1,0:T(1,128)S(1)}, f32[1,512]{1,0:T(1,128)S(1)}, bf16[16,128,1,256]{3,1,0,2:T(8,128)...) while((s32[]{:T(128)}, f32[1,512,256]{2,1,0:T(8,128)S(1)}, ...), condition=%wide.region_6.7_spmd.clone, body=%wide.region_0.6_spmd.clone.sunk | while | flops 262264704 | bytes 3193546 | solution.py:165
  113.6 1.2 multiply_add_fusion.3
  119.3 1.6 fusion.150
  121.6 1.3 fusion.147
  126.3 1.2 multiply_add_fusion.3
  132.0 1.6 fusion.150
  134.3 1.3 fusion.147
  139.0 1.2 multiply_add_fusion.3
  144.7 1.6 fusion.150
  147.0 1.3 fusion.147
  157.4 1.6 fusion.150
  159.7 1.3 fusion.147
  164.4 1.2 multiply_add_fusion.3
  170.0 1.6 fusion.150
  172.4 1.3 fusion.147
  182.7 1.6 fusion.150
  185.0 1.3 fusion.147
  195.4 1.6 fusion.150
  197.7 1.3 fusion.147
  208.1 1.6 fusion.150
  210.4 1.3 fusion.147
  215.1 1.2 multiply_add_fusion.3
  220.8 1.6 fusion.150
  223.1 1.3 fusion.147
  233.4 1.6 fusion.150
  235.8 1.3 fusion.147
  246.1 1.6 fusion.150
  248.5 1.3 fusion.147
  258.8 1.6 fusion.150
  261.1 1.3 fusion.147
  271.5 1.6 fusion.150
  273.8 1.3 fusion.147
  284.2 1.6 fusion.150
  286.5 1.3 fusion.147
  296.9 1.6 fusion.150
  299.2 1.3 fusion.147
  303.9 1.2 multiply_add_fusion.3
  309.5 1.6 fusion.150
  311.9 1.3 fusion.147
  313.8 2.7 reduce.12
  317.6 4.7 %all-to-all-start.1 = ((bf16[16,2,16384]{2,1,0:T(2,128)(2,1)}), bf16[16,2,16384]{2,1,0:T(2,128)(2,1)S(1)}, u32[]{:S(2)}, u32[]{:S(2)}) async-start(bf16[16,2,16384]{2,1,0:T(2,128)(2,1)} %reshape.468), calls=%async_computation.1 | async-start | bytes 2097152 | tf_op jit(solution)/shard_map/all_to_all | solution.py:178
  323.9 12.4 %all-to-all-done.1 = bf16[16,2,16384]{2,1,0:T(2,128)(2,1)S(1)} async-done(((bf16[16,2,16384]{2,1,0:T(2,128)(2,1)}), bf16[16,2,16384]{2,1,0:T(2,128)(2,1)S(1)}, u32[]{:S(2)}, u32[]{:S(2)}) %all-to-all-start.1) | async-done | bytes 1048608 | tf_op jit(solution)/shard_map/all_to_all | solution.py:178
  339.8 1.4 convolution_convert_fusion
  341.2 1.8 fusion.112
  343.0 27.1 %all_to_all.47 = bf16[16,16,4096]{2,1,0:T(8,128)(2,1)} all-to-all(bf16[16,16,4096]{2,1,0:T(8,128)(2,1)S(1)} %get-tuple-element.176), channel_id=1, replica_groups=mesh['seq'=16,'batch'=8] {'seq'}, dimensions={0} | all-to-all | bytes 4194304 | tf_op jit(solution)/shard_map/all_to_all | solution.py:41
  370.2 3.9 all-to-all-start.4
  374.1 5.8 %fusion.57 = f32[256,704]{0,1:T(8,128)} fusion(bf16[256,4096]{1,0:T(8,128)(2,1)} %bitcast.282, bf16[1,4096,704]{1,2,0:T(8,128)(2,1)} %param.23), kind=kOutput, calls=%fused_computation.80 | convolution fusion | flops 1476395008 | bytes 8585216 | tf_op jit(solution)/shard_map/dot_general | solution.py:207
  379.9 12.9 %fusion.59 = bf16[256,4096]{1,0:T(8,128)(2,1)} fusion(bf16[1,704,4096]{2,1,0:T(8,128)(2,1)} %param.25, bf16[256,4096]{1,0:T(8,128)(2,1)} %bitcast.283, bf16[1,4096,704]{1,2,0:T(8,128)(2,1)} %param.24, f32[256,704]{0,1:T(8,128)} %fusion.57), kind=kOutput, calls=%fused_computation.83 | convolution fusion | flops 2954919936 | bytes 16449536 | tf_op jit(solution)/shard_map/dot_general | solution.py:210
  392.8 6.0 %all-to-all-done.4 = bf16[16,16,4096]{2,1,0:T(8,128)(2,1)S(1)} async-done(((bf16[16,16,4096]{2,1,0:T(8,128)(2,1)}), bf16[16,16,4096]{2,1,0:T(8,128)(2,1)S(1)}, u32[]{:S(2)}, u32[]{:S(2)}) %all-to-all-start.4) | async-done | bytes 2097184 | tf_op jit(solution)/shard_map/all_to_all | solution.py:41
  398.7 1.3 copy-done
  400.0 3.9 all-to-all-start.3
  404.0 5.8 %fusion.55 = f32[256,704]{0,1:T(8,128)} fusion(bf16[256,4096]{1,0:T(8,128)(2,1)} %bitcast.278, bf16[1,4096,704]{1,2,0:T(8,128)(2,1)} %param.23), kind=kOutput, calls=%fused_computation.78 | convolution fusion | flops 1476395008 | bytes 8585216 | tf_op jit(solution)/shard_map/dot_general | solution.py:207
  409.8 12.8 %fusion.62 = bf16[256,4096]{1,0:T(8,128)(2,1)} fusion(bf16[1,704,4096]{2,1,0:T(8,128)(2,1)} %param.25, bf16[256,4096]{1,0:T(8,128)(2,1)} %bitcast.279, bf16[1,4096,704]{1,2,0:T(8,128)(2,1)} %param.24, f32[256,704]{0,1:T(8,128)} %fusion.55), kind=kOutput, calls=%fused_computation.84 | convolution fusion | flops 2954919936 | bytes 16449536 | tf_op jit(solution)/shard_map/dot_general | solution.py:210
  422.6 6.5 %all-to-all-done.3 = bf16[16,16,4096]{2,1,0:T(8,128)(2,1)S(1)} async-done(((bf16[16,16,4096]{2,1,0:T(8,128)(2,1)}), bf16[16,16,4096]{2,1,0:T(8,128)(2,1)S(1)}, u32[]{:S(2)}, u32[]{:S(2)}) %all-to-all-start.3) | async-done | bytes 2097184 | tf_op jit(solution)/shard_map/all_to_all | solution.py:213
  429.2 4.6 all-to-all-start.5
  433.8 24.4 %all-to-all-done.5 = bf16[16,16,4096]{2,1,0:T(8,128)(2,1)} async-done(((bf16[16,16,4096]{2,1,0:T(8,128)(2,1)}), bf16[16,16,4096]{2,1,0:T(8,128)(2,1)}, u32[]{:S(2)}, u32[]{:S(2)}) %all-to-all-start.5) | async-done | bytes 2097184 | tf_op jit(solution)/shard_map/all_to_all | solution.py:213
  458.1 2.0 pad_maximum_fusion.1
  460.9 2.1 fusion.67
  (306 shorter events, 157.4 us)
Async XLA Ops:
  0.0 1.5 copy-start.2
  0.0 1.9 copy-start.3
  5.2 7.4 %copy-start.7 = (f32[8,128]{1,0:T(8,128)S(1)}, f32[8,128]{1,0:T(8,128)}, u32[]{:S(2)}) copy-start(f32[8,128]{1,0:T(8,128)} %param.20) | copy-start | bytes 12292
  5.2 7.4 %copy-start.8 = (f32[8,128]{1,0:T(8,128)S(1)}, f32[8,128]{1,0:T(8,128)}, u32[]{:S(2)}) copy-start(f32[8,128]{1,0:T(8,128)} %param.19) | copy-start | bytes 12292
  5.2 98.9 %all-to-all-start = ((bf16[128,16,1280]{2,0,1:T(8,128)(2,1)}), bf16[128,16,1280]{2,0,1:T(8,128)(2,1)}, u32[]{:S(2)}, u32[]{:S(2)}) async-start(bf16[128,16,1280]{2,0,1:T(8,128)(2,1)} %pad_maximum_fusion), calls=%async_computation | async-start | bytes 10485760 | tf_op jit(solution)/shard_map/all_to_all | solution.py:15
  316.5 5.9 %copy-start.6 = (s32[128,2]{0,1:T(2,128)S(1)}, s32[128,2]{0,1:T(2,128)}, u32[]{:S(2)}) copy-start(s32[128,2]{0,1:T(2,128)} %param.26) | copy-start | bytes 3076
  317.6 18.7 %all-to-all-start.1 = ((bf16[16,2,16384]{2,1,0:T(2,128)(2,1)}), bf16[16,2,16384]{2,1,0:T(2,128)(2,1)S(1)}, u32[]{:S(2)}, u32[]{:S(2)}) async-start(bf16[16,2,16384]{2,1,0:T(2,128)(2,1)} %reshape.468), calls=%async_computation.1 | async-start | bytes 2097152 | tf_op jit(solution)/shard_map/all_to_all | solution.py:178
  337.9 1.2 copy-start.1
  337.9 1.2 copy-start.4
  339.1 0.7 copy-start.5
  370.2 28.6 %all-to-all-start.4 = ((bf16[16,16,4096]{2,1,0:T(8,128)(2,1)}), bf16[16,16,4096]{2,1,0:T(8,128)(2,1)S(1)}, u32[]{:S(2)}, u32[]{:S(2)}) async-start(bf16[16,16,4096]{2,1,0:T(8,128)(2,1)} %get-tuple-element.177), calls=%async_computation.4 | async-start | bytes 4194304 | tf_op jit(solution)/shard_map/all_to_all | solution.py:41
  398.7 1.3 copy-start
  400.0 29.1 %all-to-all-start.3 = ((bf16[16,16,4096]{2,1,0:T(8,128)(2,1)}), bf16[16,16,4096]{2,1,0:T(8,128)(2,1)S(1)}, u32[]{:S(2)}, u32[]{:S(2)}) async-start(bf16[16,16,4096]{2,1,0:T(8,128)(2,1)} %bitcast.280), calls=%async_computation.3 | async-start | bytes 4194304 | tf_op jit(solution)/shard_map/all_to_all | solution.py:213
  429.2 4.6 copy-start.9
  429.2 29.0 %all-to-all-start.5 = ((bf16[16,16,4096]{2,1,0:T(8,128)(2,1)}), bf16[16,16,4096]{2,1,0:T(8,128)(2,1)}, u32[]{:S(2)}, u32[]{:S(2)}) async-start(bf16[16,16,4096]{2,1,0:T(8,128)(2,1)} %bitcast.281), calls=%async_computation.5 | async-start | bytes 4194304 | tf_op jit(solution)/shard_map/all_to_all | solution.py:213
where the time goes:
time: 467 us; the launch traced here: 463 us
  matrix products  138 us (30%)
  blocking collectives  119 us (25%)
  other arithmetic  85.7 us (18%)
  waiting for transfers between devices  49.3 us (11%)
  local copies, waits for them, and re-layouts  45.2 us (10%)
  starting transfers between devices  24.4 us (5%)
    all_gather x1, blocking collectives, side_by_side(): lax.all_gather(both, axis, axis=dim, tiled=True)  91.4 us
    all_to_all x2, waiting for transfers between devices, run_expert(): lax.all_to_all(result.reshape(block_in.shape), 'seq', split_axis=0, conca...  30.9 us
    all_to_all x1, blocking collectives, items_in_groups(): lax.all_to_all(group, axis, split_axis=split_dim, concat_axis=concat_dim,...  27.1 us
    dot_general x2, matrix products, run_expert(): jnp.dot(hidden, expert_down[0], preferred_element_type=jnp.float32)  25.7 us
    dot_general x16, matrix products, block_mix(): jnp.einsum('thd,hde->the', query_float, carry_state, precision=lax.Precis...  25.2 us
    dot_general x16, matrix products, block_state(): jnp.einsum('thd,the->hde', rounded, values_three, preferred_element_type=...  20.2 us
    add x16, other arithmetic, join_states(): normv_new = scale_early * normv_early + scale_late * normv_late  19.4 us
    exp x16, other arithmetic, block_state(): weight = jnp.exp(tail_log - peak_tail[:, None])  19.2 us
  transfers between devices with their start and end apart: 5, of which 4 were waited for; matrix products, arithmetic and copies ran while one was open for 8% of the time, Pallas kernels for 0%

commit v1 on v0

v1 whole, which is shorter than its diff:
```python
import functools
import math

import jax
import jax.numpy as jnp
from jax import lax
from jax.experimental import pallas as pl
from jax.experimental.pallas import tpu as pltpu
from jax.sharding import PartitionSpec as P

NEG_FILL = -1e30
EPSILON = 1e-06
MESH = pl.DeviceIdType.MESH
HEADS = 8
DH = 512
D = 4096
FF = 704
TOK = 128
CAP = 32
DEV = 16
CHUNK = 256
ROOT = 1.0 / math.sqrt(DH)
ORDER = (0, 1, 3, 4, 12, 2, 8, 10, 5, 15, 7, 13, 6, 14, 9, 11)
NEAR = ((0, 1), (0, 3), (1, 0), (1, 1), (1, 3), (0, 2), (1, 2))


def peer_of(me, offset):
    row = lax.rem(me // 4 + offset // 4, 4)
    col = lax.rem(lax.rem(me, 4) + offset % 4, 4)
    return row * 4 + col


def entry_barrier(me):
    barrier = pltpu.get_barrier_semaphore()
    for offset in range(1, DEV):
        pl.semaphore_signal(
            barrier, inc=1, device_id={"seq": peer_of(me, offset)}, device_id_type=MESH
        )
    pl.semaphore_wait(barrier, DEV - 1)


def remote(src, dst, send, recv, device):
    return pltpu.make_async_remote_copy(
        src_ref=src,
        dst_ref=dst,
        send_sem=send,
        recv_sem=recv,
        device_id={"seq": device},
        device_id_type=MESH,
    )


def scan_lanes(x, op, fill):
    lane = lax.broadcasted_iota(jnp.int32, x.shape, 1)
    step = 1
    while step < x.shape[1]:
        x = op(x, jnp.where(lane >= step, pltpu.roll(x, step, 1), fill))
        step *= 2
    return x


def three_parts(x):
    high = x.astype(jnp.bfloat16).astype(jnp.float32)
    rest = x - high
    middle = rest.astype(jnp.bfloat16).astype(jnp.float32)
    return high, middle, rest - middle


def nt_dot(a, b):
    return lax.dot_general(a, b, (((1,), (1,)), ((), ())), preferred_element_type=jnp.float32)


def mixer_kernel(
    q_in, k_in, v_in, gate_i, gate_f, mix,
    qb, kb, vb, gbi, gbf, chi, clo, sacc, zst, z_in, st_in, st_out, z_out, ob, rowi, rowf, grow, tcol,
    own_sem, gs, gr, ks, kr, vs, vr, qs, qr, os, orr, ss, sr,
):
    me = lax.axis_index("seq")
    half = me // 8
    base = half * 8
    local = me - base
    head = lax.rem(local + 4 * half, 8)

    def rows(j):
        return pl.ds(pl.multiple_of(j * TOK, TOK), TOK)

    def head_columns(h):
        return pl.ds(pl.multiple_of(h * DH, DH), DH)

    own = [
        pltpu.make_async_copy(src.at[:, head_columns(head)], dst.at[rows(local), :], own_sem.at[n])
        for n, (src, dst) in enumerate(((k_in, kb), (v_in, vb), (q_in, qb)))
    ]
    for copy in own:
        copy.start()
    entry_barrier(me)

    sent = []
    for offset in range(1, DEV):
        to = peer_of(me, offset)
        for src, dst, n in ((gate_i, gbi, 0), (gate_f, gbf, 1)):
            copy = remote(src, dst.at[me], gs.at[n, offset], gr.at[n, me], to)
            copy.start()
            sent.append(copy)
    gbi[me] = gate_i[...]
    gbf[me] = gate_f[...]

    def send_all(src, dst, send, recv):
        for n, (dy, dx) in enumerate(NEAR):
            to = lax.rem(local // 4 + dy, 2) * 4 + lax.rem(lax.rem(local, 4) + dx, 4)
            to_head = lax.rem(to + 4 * half, 8)
            copy = remote(
                src.at[:, head_columns(to_head)], dst.at[rows(local), :], send.at[n], recv.at[local], base + to
            )
            copy.start()
            sent.append(copy)

    send_all(k_in, kb, ks, kr)
    send_all(v_in, vb, vs, vr)
    send_all(q_in, qb, qs, qr)

    for offset in range(1, DEV):
        src = peer_of(me, offset)
        remote(gate_i, gbi.at[src], gs.at[0, offset], gr.at[0, src], me).wait_recv()
        remote(gate_f, gbf.at[src], gs.at[1, offset], gr.at[1, src], me).wait_recv()
    for b in range(DEV):
        rowi[b // 2 : b // 2 + 1, (b % 2) * TOK : (b % 2 + 1) * TOK] = gbi[b, pl.ds(head, 1), :]
        rowf[b // 2 : b // 2 + 1, (b % 2) * TOK : (b % 2 + 1) * TOK] = gbf[b, pl.ds(head, 1), :]
    x = rowf[...]
    log_forget = jnp.minimum(x, 0.0) - jnp.log1p(jnp.exp(-jnp.abs(x)))
    cumul = scan_lanes(log_forget, jnp.add, 0.0)
    lift = rowi[...] - cumul
    lift_max = scan_lanes(lift, jnp.maximum, NEG_FILL)
    decay = cumul[:, CHUNK - 1 : CHUNK]
    peak_in = decay + lift_max[:, CHUNK - 1 : CHUNK]
    peaks = [jnp.full((1, 1), NEG_FILL, jnp.float32)]
    for c in range(8):
        peaks.append(jnp.maximum(decay[c : c + 1] + peaks[-1], peak_in[c : c + 1]))
    first = half == 0
    scales = []
    since = jnp.ones((1, 1), jnp.float32)
    row8 = lax.broadcasted_iota(jnp.int32, (8, CHUNK), 0)
    for c in range(4):
        before = jnp.where(first, peaks[c], peaks[4 + c])
        after = jnp.where(first, peaks[c + 1], peaks[5 + c])
        dec = jnp.where(first, decay[c : c + 1], decay[4 + c : 5 + c])
        lift_c = jnp.where(first, lift[c : c + 1], lift[4 + c : 5 + c])
        top = jnp.maximum(jnp.where(first, lift_max[c : c + 1], lift_max[4 + c : 5 + c]), before)
        weight = jnp.exp(dec + lift_c - after)
        reach = jnp.exp(before - top) * ROOT
        packed = jnp.where(
            row8 == 0, weight, jnp.where(row8 == 1, top, jnp.where(row8 == 2, reach, reach * since))
        )
        tcol[c] = jnp.transpose(packed)
        grow[c] = lift_c
        scales.append(jnp.exp(dec + before - after))
        since = since * scales[-1]

    for c in range(4):
        for j in (2 * c, 2 * c + 1):

            @pl.when(j != local)
            def _():
                remote(kb.at[rows(j), :], kb.at[rows(j), :], ks.at[0], kr.at[j], me).wait_recv()
                remote(vb.at[rows(j), :], vb.at[rows(j), :], vs.at[0], vr.at[j], me).wait_recv()

            @pl.when(j == local)
            def _():
                own[0].wait()
                own[1].wait()

        weighted = kb[c * CHUNK : (c + 1) * CHUNK, :].astype(jnp.float32) * tcol[c][:, 0:1]
        fresh = lax.dot_general(
            weighted.astype(jnp.bfloat16),
            vb[c * CHUNK : (c + 1) * CHUNK, :],
            (((0,), (0,)), ((), ())),
            preferred_element_type=jnp.float32,
        )
        fresh_z = jnp.sum(weighted, axis=0, keepdims=True)
        if c == 0:
            chi[0] = jnp.zeros((DH, DH), jnp.bfloat16)
            clo[0] = jnp.zeros((DH, DH), jnp.bfloat16)
            zst[0] = jnp.zeros((1, DH), jnp.float32)
            z_now = fresh_z
            state = fresh
        else:
            state = scales[c] * sacc[...] + fresh
            z_now = scales[c] * z_now + fresh_z
        high = state.astype(jnp.bfloat16)
        if c < 3:
            sacc[...] = state
            zst[c + 1] = z_now
            chi[c + 1] = high
            clo[c + 1] = (state - high.astype(jnp.float32)).astype(jnp.bfloat16)
        else:
            st_out[...] = high
            z_out[...] = jnp.broadcast_to(z_now, (8, DH))

    next_device = 8 + lax.rem(local + 4, 8)
    state_copy = remote(st_out, st_in, ss.at[0], sr.at[0], next_device)
    z_copy = remote(z_out, z_in, ss.at[1], sr.at[1], next_device)

    @pl.when(half == 0)
    def _():
        state_copy.start()
        z_copy.start()
        z_in[...] = jnp.zeros((8, DH), jnp.float32)

    @pl.when(half == 1)
    def _():
        state_copy.wait_recv()
        z_copy.wait_recv()

    causal = lax.broadcasted_iota(jnp.int32, (CHUNK, CHUNK), 0) >= lax.broadcasted_iota(
        jnp.int32, (CHUNK, CHUNK), 1
    )
    z_row = lax.broadcasted_iota(jnp.int32, (8, DH), 0)

    @pl.loop(0, 4)
    def _(i):
        c = lax.rem(i + 1 + local // 2, 4)
        for jj in range(2):
            j = 2 * c + jj

            @pl.when(j != local)
            def _():
                remote(qb.at[rows(j), :], qb.at[rows(j), :], qs.at[0], qr.at[j], me).wait_recv()

            @pl.when(j == local)
            def _():
                own[2].wait()

        part = pl.ds(pl.multiple_of(c * CHUNK, CHUNK), CHUNK)
        query = qb[part, :]
        value = vb[part, :]
        columns = tcol[c]
        top, reach, reach0 = columns[:, 1:2], columns[:, 2:3], columns[:, 3:4]
        weight = jnp.exp(jnp.where(causal, grow[c] - top, NEG_FILL))
        coef = weight * (nt_dot(query, kb[part, :]) * ROOT)
        denom = jnp.sum(coef, axis=1, keepdims=True)
        numer = jnp.dot(coef.astype(jnp.bfloat16), value, preferred_element_type=jnp.float32)
        held = jnp.dot(query, chi[c], preferred_element_type=jnp.float32)
        held += jnp.dot(query, clo[c], preferred_element_type=jnp.float32)
        parts = three_parts(zst[c]) + three_parts(z_in[0:1, :])
        z_all = jnp.zeros((8, DH), jnp.float32)
        for n, piece in enumerate(parts):
            z_all = jnp.where(z_row == n, piece, z_all)
        norm = nt_dot(query, z_all.astype(jnp.bfloat16))
        denom += reach * (norm[:, 0:1] + norm[:, 1:2] + norm[:, 2:3])
        denom += reach0 * (norm[:, 3:4] + norm[:, 4:5] + norm[:, 5:6])
        numer += reach * held

        def finish(total):
            ob[part, :] = (total / jnp.maximum(jnp.abs(denom), 1.0)).astype(jnp.bfloat16)

        @pl.when(half == 0)
        def _():
            finish(numer)

        @pl.when(half == 1)
        def _():
            finish(numer + reach0 * jnp.dot(query, st_in[...], preferred_element_type=jnp.float32))

        for jj in range(2):
            j = 2 * c + jj

            @pl.when(j != local)
            def _():
                remote(ob.at[rows(j), :], mix.at[head], os.at[j], orr.at[head], base + j).start()

            @pl.when(j == local)
            def _():
                mix[head] = ob[rows(j), :]

    for copy in sent:
        copy.wait_send()

    @pl.when(half == 0)
    def _():
        state_copy.wait_send()
        z_copy.wait_send()

    for j in range(8):

        @pl.when(j != local)
        def _():
            from_head = lax.rem(j + 4 * half, 8)
            copy = remote(ob.at[rows(j), :], mix.at[from_head], os.at[j], orr.at[from_head], me)
            copy.wait_send()
            copy.wait_recv()


def expert_kernel(
    mix, residual, mix_gain, ffn_gain, routes, route_weight, w_gate, w_up, w_down, out,
    gate_v, up_v, down_v, disp, inbox, result, back, upd, normed, wmat, acc,
    w_sem, ds, dr, bs, br,
):
    me = lax.axis_index("seq")
    weights = [
        pltpu.make_async_copy(src, dst, w_sem.at[n])
        for n, (src, dst) in enumerate(((w_gate, gate_v), (w_up, up_v), (w_down, down_v)))
    ]
    for copy in weights:
        copy.start()
    entry_barrier(me)

    owner = jnp.zeros((DEV, TOK), jnp.int32)
    row16 = lax.broadcasted_iota(jnp.int32, (DEV, TOK), 0)
    for n, offset in enumerate(ORDER):
        owner = jnp.where(row16 == n, peer_of(me, offset), owner)
    hit0 = routes[0:1, :] == owner
    hit1 = routes[1:2, :] == owner
    match = jnp.where(hit0 | hit1, 1.0, 0.0).astype(jnp.bfloat16)
    earlier = lax.broadcasted_iota(jnp.int32, (TOK, TOK), 0) < lax.broadcasted_iota(
        jnp.int32, (TOK, TOK), 1
    )
    position = jnp.dot(
        match, jnp.where(earlier, 1.0, 0.0).astype(jnp.bfloat16), preferred_element_type=jnp.float32
    )
    slot = position + (row16 * CAP).astype(jnp.float32)
    slot0 = jnp.sum(jnp.where(hit0, slot, 0.0), axis=0, keepdims=True)
    slot1 = jnp.sum(jnp.where(hit1, slot, 0.0), axis=0, keepdims=True)
    row8 = lax.broadcasted_iota(jnp.int32, (8, TOK), 0)
    packed = jnp.where(
        row8 == 0,
        slot0,
        jnp.where(row8 == 1, slot1, jnp.where(row8 == 2, route_weight[0:1, :], route_weight[1:2, :])),
    )
    columns = jnp.transpose(packed)
    lane = lax.broadcasted_iota(jnp.int32, (TOK, DEV * CAP), 1).astype(jnp.float32)
    share = jnp.where(lane == columns[:, 0:1], columns[:, 2:3], 0.0) + jnp.where(
        lane == columns[:, 1:2], columns[:, 3:4], 0.0
    )
    high = share.astype(jnp.bfloat16)
    low = (share - high.astype(jnp.float32)).astype(jnp.bfloat16)
    for g in range(4):
        wmat[g, 0:TOK, :] = high[:, g * TOK : (g + 1) * TOK]
        wmat[g, TOK : 2 * TOK, :] = low[:, g * TOK : (g + 1) * TOK]

    square = jnp.zeros((TOK, 1), jnp.float32)
    for h in range(HEADS):
        part = mix[h].astype(jnp.float32)
        square += jnp.sum(part * part, axis=1, keepdims=True)
    scale = lax.rsqrt(square * (1.0 / D) + EPSILON)
    square = jnp.zeros((TOK, 1), jnp.float32)
    for h in range(HEADS):
        cols = slice(h * DH, (h + 1) * DH)
        part = residual[:, cols].astype(jnp.float32) + mix[h].astype(jnp.float32) * scale * mix_gain[:, cols]
        rounded = part.astype(jnp.bfloat16)
        upd[:, cols] = rounded
        part = rounded.astype(jnp.float32)
        square += jnp.sum(part * part, axis=1, keepdims=True)
    scale = lax.rsqrt(square * (1.0 / D) + EPSILON)
    for h in range(HEADS):
        cols = slice(h * DH, (h + 1) * DH)
        part = upd[:, cols].astype(jnp.float32)
        acc[:, cols] = part
        normed[:, cols] = (part * scale * ffn_gain[:, cols]).astype(jnp.bfloat16)

    pieces = 4
    depth = CAP // pieces
    for g in range(4):
        target = lax.broadcasted_iota(jnp.int32, (TOK, TOK), 0) + g * TOK
        pick = jnp.where((target == slot0.astype(jnp.int32)) | (target == slot1.astype(jnp.int32)), 1.0, 0.0)
        pick = pick.astype(jnp.bfloat16)
        for h in range(HEADS):
            cols = slice(h * DH, (h + 1) * DH)
            rows = jnp.dot(pick, normed[:, cols], preferred_element_type=jnp.float32)
            disp[g * TOK : (g + 1) * TOK, cols] = rows.astype(jnp.bfloat16)
        for p in range(pieces):
            for n in range(4 * g, 4 * g + 4):
                if n == 0:
                    continue
                piece = pl.ds(n * CAP + p * depth, depth)
                remote(
                    disp.at[piece, :], inbox.at[piece, :], ds.at[n], dr.at[n], peer_of(me, ORDER[n])
                ).start()
    inbox[0:CAP, :] = disp[0:CAP, :]

    def slot_rows(n):
        return pl.ds(n * CAP, CAP)

    for copy in weights:
        copy.wait()

    for g in range(4):
        for n in range(4 * g, 4 * g + 4):
            if n > 0:
                remote(disp.at[slot_rows(n), :], inbox.at[slot_rows(n), :], ds.at[n], dr.at[n], me).wait_recv()
        if g == 0:
            pass
        rows = inbox[g * TOK : (g + 1) * TOK, :]
        gate = nt_dot(rows, gate_v[...])
        up = nt_dot(rows, up_v[...])
        hidden = (gate / (1.0 + jnp.exp(-gate)) * up).astype(jnp.bfloat16)
        for h in range(HEADS):
            cols = slice(h * DH, (h + 1) * DH)
            result[g * TOK : (g + 1) * TOK, cols] = jnp.dot(
                hidden, down_v[:, cols], preferred_element_type=jnp.float32
            ).astype(jnp.bfloat16)
        for p in range(pieces):
            for n in range(4 * g, 4 * g + 4):
                if n == 0:
                    continue
                piece = pl.ds(n * CAP + p * depth, depth)
                back_to = peer_of(me, (4 - ORDER[n] // 4) % 4 * 4 + (4 - ORDER[n] % 4) % 4)
                remote(result.at[piece, :], back.at[piece, :], bs.at[n], br.at[n], back_to).start()
    back[0:CAP, :] = result[0:CAP, :]

    for g in range(4):
        for n in range(4 * g, 4 * g + 4):
            if n > 0:
                remote(result.at[slot_rows(n), :], back.at[slot_rows(n), :], bs.at[n], br.at[n], me).wait_recv()
        for h in range(HEADS):
            cols = slice(h * DH, (h + 1) * DH)
            both = jnp.dot(wmat[g], back[g * TOK : (g + 1) * TOK, cols], preferred_element_type=jnp.float32)
            total = acc[:, cols] + both[0:TOK, :] + both[TOK : 2 * TOK, :]
            if g < 3:
                acc[:, cols] = total
            else:
                out[:, cols] = total.astype(jnp.bfloat16)
    for n in range(1, DEV):
        remote(disp.at[slot_rows(n), :], inbox.at[slot_rows(n), :], ds.at[n], dr.at[n], me).wait_send()
        remote(result.at[slot_rows(n), :], back.at[slot_rows(n), :], bs.at[n], br.at[n], me).wait_send()


def shards(
    queries, key_vectors, value_vectors, residual_in, input_logit, forget_logit, mix_gain, ffn_gain,
    expert_gate, expert_up, expert_down, routes, route_weight,
):
    vmem = pl.BlockSpec(memory_space=pltpu.VMEM)
    hbm = pl.BlockSpec(memory_space=pl.ANY)
    dma = pltpu.SemaphoreType.DMA
    bf16, f32 = jnp.bfloat16, jnp.float32
    mixed = pl.pallas_call(
        mixer_kernel,
        out_shape=jax.ShapeDtypeStruct((HEADS, TOK, DH), bf16),
        in_specs=[hbm, hbm, hbm, vmem, vmem],
        out_specs=vmem,
        scratch_shapes=[
            pltpu.VMEM((8 * TOK, DH), bf16),
            pltpu.VMEM((8 * TOK, DH), bf16),
            pltpu.VMEM((8 * TOK, DH), bf16),
            pltpu.VMEM((DEV, HEADS, TOK), f32),
            pltpu.VMEM((DEV, HEADS, TOK), f32),
            pltpu.VMEM((4, DH, DH), bf16),
            pltpu.VMEM((4, DH, DH), bf16),
            pltpu.VMEM((DH, DH), f32),
            pltpu.VMEM((4, 1, DH), f32),
            pltpu.VMEM((8, DH), f32),
            pltpu.VMEM((DH, DH), bf16),
            pltpu.VMEM((DH, DH), bf16),
            pltpu.VMEM((8, DH), f32),
            pltpu.VMEM((8 * TOK, DH), bf16),
            pltpu.VMEM((8, CHUNK), f32),
            pltpu.VMEM((8, CHUNK), f32),
            pltpu.VMEM((4, 1, CHUNK), f32),
            pltpu.VMEM((4, CHUNK, 8), f32),
            dma((3,)),
            dma((2, DEV)),
            dma((2, DEV)),
            dma((7,)),
            dma((8,)),
            dma((7,)),
            dma((8,)),
            dma((7,)),
            dma((8,)),
            dma((8,)),
            dma((8,)),
            dma((2,)),
            dma((2,)),
        ],
        compiler_params=pltpu.CompilerParams(
            collective_id=0, has_side_effects=True, vmem_limit_bytes=60 << 20
        ),
        name="mixer",
    )(queries, key_vectors, value_vectors, input_logit, forget_logit)
    return pl.pallas_call(
        expert_kernel,
        out_shape=jax.ShapeDtypeStruct((TOK, D), bf16),
        in_specs=[vmem] * 6 + [hbm] * 3,
        out_specs=vmem,
        scratch_shapes=[
            pltpu.VMEM((FF, D), bf16),
            pltpu.VMEM((FF, D), bf16),
            pltpu.VMEM((FF, D), bf16),
            pltpu.VMEM((DEV * CAP, D), bf16),
            pltpu.VMEM((DEV * CAP, D), bf16),
            pltpu.VMEM((DEV * CAP, D), bf16),
            pltpu.VMEM((DEV * CAP, D), bf16),
            pltpu.VMEM((TOK, D), bf16),
            pltpu.VMEM((TOK, D), bf16),
            pltpu.VMEM((4, 2 * TOK, TOK), bf16),
            pltpu.VMEM((TOK, D), f32),
            dma((3,)),
            dma((DEV,)),
            dma((DEV,)),
            dma((DEV,)),
            dma((DEV,)),
        ],
        compiler_params=pltpu.CompilerParams(
            collective_id=1, has_side_effects=True, vmem_limit_bytes=60 << 20
        ),
        name="experts",
    )(
        mixed,
        residual_in,
        mix_gain.reshape(1, D),
        ffn_gain.reshape(1, D),
        jnp.transpose(routes),
        jnp.transpose(route_weight),
        jnp.swapaxes(expert_gate[0], 0, 1),
        jnp.swapaxes(expert_up[0], 0, 1),
        expert_down[0],
    )


def solution(mesh):
    return jax.shard_map(
        shards,
        mesh=mesh,
        in_specs=(
            P(("batch", "seq"), None),
            P(("batch", "seq"), None),
            P(("batch", "seq"), None),
            P(("batch", "seq"), None),
            P(None, ("batch", "seq")),
            P(None, ("batch", "seq")),
            P(),
            P(),
            P("seq", None, None),
            P("seq", None, None),
            P("seq", None, None),
            P(("batch", "seq"), None),
            P(("batch", "seq"), None),
        ),
        out_specs=P(("batch", "seq"), None),
        check_vma=False,
    )
```

time: 467 us -> 168 us (0.36)
  Pallas kernels: 0 us -> 165 us
  matrix products: 138 us -> 0 us
  blocking collectives: 119 us -> 0 us
  other arithmetic: 85.7 us -> 0 us
  waiting for transfers between devices: 49.3 us -> 0 us
  local copies, waits for them, and re-layouts: 45.2 us -> 2.29 us
  starting transfers between devices: 24.4 us -> 0 us
    pallas_call x0 -> x2, Pallas kernels: none -> 165 us  [the longest x1 105 us: shards(): pl.pallas_call(expert_kernel, out_shape=jax.ShapeDtypeStruct((TOK, D), bf...]
    dot_general x87 -> x0, matrix products: 138 us -> none  [the longest x2 25.7 us: run_expert(): jnp.dot(hidden, expert_down[0], preferred_element_type=jnp.float32)]
    all_gather x1 -> x0, blocking collectives: 91.4 us -> none  [side_by_side(): lax.all_gather(both, axis, axis=dim, tiled=True)]
    all_to_all x5 -> x0, waiting for transfers between devices: 49.3 us -> none  [the longest x2 30.9 us: run_expert(): lax.all_to_all(result.reshape(block_in.shape), 'seq', split_axis=0, conca...]
    all_to_all x1 -> x0, blocking collectives: 27.1 us -> none  [items_in_groups(): lax.all_to_all(group, axis, split_axis=split_dim, concat_axis=concat_dim,...]
    all_to_all x5 -> x0, starting transfers between devices: 24.4 us -> none  [the longest x2 8.49 us: run_expert(): lax.all_to_all(result.reshape(block_in.shape), 'seq', split_axis=0, conca...]
    reduce_max x32 -> x0, other arithmetic: 21.7 us -> none  [the longest x16 18.9 us: block_state(): peak_tail = jnp.max(tail_log, axis=1)]
    add x17 -> x0, other arithmetic: 19.4 us -> none  [the longest x16 19.4 us: join_states(): normv_new = scale_early * normv_early + scale_late * normv_late]
  transfers between devices with their start and end apart: 5 -> 0, of which waited for: 4 -> 0; matrix products, arithmetic and copies ran while one was open for 8% -> 0% of each run, Pallas kernels for 0% -> 0%
where the time goes in v1:
time: 168 us; the launch traced here: 167 us
  Pallas kernels  165 us (98%)
  local copies, waits for them, and re-layouts  2.29 us (1%)
    pallas_call x1, Pallas kernels, shards(): pl.pallas_call(expert_kernel, out_shape=jax.ShapeDtypeStruct((TOK, D), bf...  105 us
    pallas_call x1, Pallas kernels, shards(): pl.pallas_call(mixer_kernel, out_shape=jax.ShapeDtypeStruct((HEADS, TOK,...  59.6 us

profile of v1, /device:TPU:0, one launch (start us, length us, event | category | flops | bytes accessed | tf_op | source)
XLA Modules:
  0.0 167.0 jit_solution(9448378704141523762)
XLA Ops:
  0.0 59.6 %mixer.1.mix = bf16[8,128,512]{2,1,0:T(8,128)(2,1)} custom-call(bf16[128,4096]{1,0:T(8,128)(2,1)} %q_in.1, bf16[128,4096]{1,0:T(8,128)(2,1)} %k_in.1, bf16[128,4096]{1,0:T(8,128)(2,1)} %v_in.1, f32[8,128]{1,0:T(8,128)} %gate_i.1, f32[8,128]{1,0:T(8,128)} %gate_f.1), custom_call_target="tpu_custom_call" | custom-call | tf_op jit(solution)/shard_map/mixer/pallas_call | solution.py:435
  59.6 105.2 %experts.1 = bf16[128,4096]{1,0:T(8,128)(2,1)} custom-call(bf16[8,128,512]{2,1,0:T(8,128)(2,1)} %mixer.1.mix, bf16[128,4096]{1,0:T(8,128)(2,1)} %residual.1, f32[1,4096]{1,0:T(1,128)} %bitcast.14, f32[1,4096]{1,0:T(1,128)} %bitcast.15, s32[2,128]{1,0:T(2,128)} %bitcast.16, f32[2,128]{1,0:T(2,128)} %bitcast.17, bf16[704,4096]{1,0:T(8,128)(2,1)} %bitcast.11, ...), custom_call_target="tpu_custom_call" | custom-call | tf_op jit(solution)/shard_map/experts/pallas_call | solution.py:478
  164.7 2.3 %copy.15 = bf16[128,4096]{1,0:T(8,128)(2,1)} copy(bf16[128,4096]{1,0:T(8,128)(2,1)} %experts.1) | data formatting | bytes 2097152

commit v2 on v1

v2 whole, which is shorter than its diff:
```python
import functools
import math

import jax
import jax.numpy as jnp
from jax import lax
from jax.experimental import pallas as pl
from jax.experimental.pallas import tpu as pltpu
from jax.sharding import PartitionSpec as P

NEG_FILL = -1e30
EPSILON = 1e-06
MESH = pl.DeviceIdType.MESH
HEADS = 8
DH = 512
D = 4096
FF = 704
TOK = 128
CAP = 32
DEV = 16
CHUNK = 256
ROOT = 1.0 / math.sqrt(DH)
ORDER = (0, 1, 3, 4, 12, 2, 8, 10, 5, 15, 7, 13, 6, 14, 9, 11)
NEAR = ((0, 1), (0, 3), (1, 0), (1, 1), (1, 3), (0, 2), (1, 2))


def peer_of(me, offset):
    row = lax.rem(me // 4 + offset // 4, 4)
    col = lax.rem(lax.rem(me, 4) + offset % 4, 4)
    return row * 4 + col


def entry_barrier(me):
    barrier = pltpu.get_barrier_semaphore()
    for offset in range(1, DEV):
        pl.semaphore_signal(
            barrier, inc=1, device_id={"seq": peer_of(me, offset)}, device_id_type=MESH
        )
    pl.semaphore_wait(barrier, DEV - 1)


def remote(src, dst, send, recv, device):
    return pltpu.make_async_remote_copy(
        src_ref=src,
        dst_ref=dst,
        send_sem=send,
        recv_sem=recv,
        device_id={"seq": device},
        device_id_type=MESH,
    )


def scan_lanes(x, op, fill):
    lane = lax.broadcasted_iota(jnp.int32, x.shape, 1)
    step = 1
    while step < x.shape[1]:
        x = op(x, jnp.where(lane >= step, pltpu.roll(x, step, 1), fill))
        step *= 2
    return x


def three_parts(x):
    high = x.astype(jnp.bfloat16).astype(jnp.float32)
    rest = x - high
    middle = rest.astype(jnp.bfloat16).astype(jnp.float32)
    return high, middle, rest - middle


def nt_dot(a, b):
    return lax.dot_general(a, b, (((1,), (1,)), ((), ())), preferred_element_type=jnp.float32)


def kernel(
    q_in, k_in, v_in, gate_i, gate_f, residual_in, gain_m, gain_f, routes_in, share_in, w_gate, w_up, w_down, out,
    qb, kb, vb, kwt, gbi, gbf, chi, clo, sacc, zst, z_in, st_in, st_out, z_out, ob, mix, rowi, rowf, grow, tcol,
    residual, mix_gain, ffn_gain, routes, route_weight,
    gate_v, up_v, down_v, disp, inbox, result, back, upd, normed, picks, wmat, acc,
    own_sem, w_sem, gs, gr, ks, kr, vs, vr, qs, qr, os, orr, ss, sr, ds, dr, bs, br,
):
    me = lax.axis_index("seq")
    half = me // 8
    base = half * 8
    local = me - base
    pair = local // 2
    head = lax.rem(local + 4 * half, 8)

    def rows(j):
        return pl.ds(pl.multiple_of(j * TOK, TOK), TOK)

    def head_columns(h):
        return pl.ds(pl.multiple_of(h * DH, DH), DH)

    own = [
        pltpu.make_async_copy(src.at[:, head_columns(head)], dst, own_sem.at[n])
        for n, (src, dst) in enumerate(
            ((k_in, kb.at[rows(local), :]), (v_in, vb.at[rows(local), :]), (q_in, qb.at[rows(local), :]))
        )
    ]
    own_gates = [
        pltpu.make_async_copy(gate_i, gbi.at[me], own_sem.at[3]),
        pltpu.make_async_copy(gate_f, gbf.at[me], own_sem.at[4]),
    ]
    fetched = [
        pltpu.make_async_copy(src, dst, w_sem.at[n])
        for n, (src, dst) in enumerate(
            (
                (routes_in, routes),
                (share_in, route_weight),
                (gain_m, mix_gain),
                (gain_f, ffn_gain),
                (residual_in, residual),
                (w_gate, gate_v),
                (w_up, up_v),
                (w_down, down_v),
            )
        )
    ]
    for copy in own + own_gates + fetched:
        copy.start()
    entry_barrier(me)

    sent = []
    for offset in range(1, DEV):
        to = peer_of(me, offset)
        for src, dst, n in ((gate_i, gbi, 0), (gate_f, gbf, 1)):
            copy = remote(src, dst.at[me], gs.at[n, offset], gr.at[n, me], to)
            copy.start()
            sent.append(copy)

    def send_part(src, dst, send, recv, lo, width, to):
        to_head = lax.rem(to + 4 * half, 8)
        part = pl.ds(pl.multiple_of(to_head * DH + lo, width), width)
        copy = remote(src.at[:, part], dst.at[rows(local), lo : lo + width], send, recv, base + to)
        copy.start()
        sent.append(copy)

    for src, dst, send, recv in ((k_in, kb, ks, kr), (v_in, vb, vs, vr)):
        for part in range(2):
            for n, (dy, dx) in enumerate(NEAR):
                to = lax.rem(local // 4 + dy, 2) * 4 + lax.rem(lax.rem(local, 4) + dx, 4)
                send_part(src, dst, send.at[part, n], recv.at[part, local], part * 256, 256, to)
    for n in range(7):
        if n < 6:
            to = 2 * lax.rem(pair + 3 - n // 2, 4) + n % 2
        else:
            to = 2 * pair + 1 - lax.rem(local, 2)
        send_part(q_in, qb, qs.at[n], qr.at[local], 0, DH, to)

    for n in range(4):
        fetched[n].wait()
    owner = jnp.zeros((DEV, TOK), jnp.int32)
    row16 = lax.broadcasted_iota(jnp.int32, (DEV, TOK), 0)
    for n, offset in enumerate(ORDER):
        owner = jnp.where(row16 == n, peer_of(me, offset), owner)
    hit0 = routes[0:1, :] == owner
    hit1 = routes[1:2, :] == owner
    match = jnp.where(hit0 | hit1, 1.0, 0.0).astype(jnp.bfloat16)
    earlier = lax.broadcasted_iota(jnp.int32, (TOK, TOK), 0) < lax.broadcasted_iota(
        jnp.int32, (TOK, TOK), 1
    )
    position = jnp.dot(
        match, jnp.where(earlier, 1.0, 0.0).astype(jnp.bfloat16), preferred_element_type=jnp.float32
    )
    slot = position + (row16 * CAP).astype(jnp.float32)
    slot0 = jnp.sum(jnp.where(hit0, slot, 0.0), axis=0, keepdims=True)
    slot1 = jnp.sum(jnp.where(hit1, slot, 0.0), axis=0, keepdims=True)
    row8 = lax.broadcasted_iota(jnp.int32, (8, TOK), 0)
    packed = jnp.where(
        row8 == 0,
        slot0,
        jnp.where(row8 == 1, slot1, jnp.where(row8 == 2, route_weight[0:1, :], route_weight[1:2, :])),
    )
    columns = jnp.transpose(packed)
    lane = lax.broadcasted_iota(jnp.int32, (TOK, DEV * CAP), 1).astype(jnp.float32)
    share = jnp.where(lane == columns[:, 0:1], columns[:, 2:3], 0.0) + jnp.where(
        lane == columns[:, 1:2], columns[:, 3:4], 0.0
    )
    high = share.astype(jnp.bfloat16)
    low = (share - high.astype(jnp.float32)).astype(jnp.bfloat16)
    for g in range(4):
        wmat[g, 0:TOK, :] = high[:, g * TOK : (g + 1) * TOK]
        wmat[g, TOK : 2 * TOK, :] = low[:, g * TOK : (g + 1) * TOK]
        target = lax.broadcasted_iota(jnp.int32, (TOK, TOK), 0) + g * TOK
        pick = jnp.where((target == slot0.astype(jnp.int32)) | (target == slot1.astype(jnp.int32)), 1.0, 0.0)
        picks[g] = pick.astype(jnp.bfloat16)

    for copy in own_gates:
        copy.wait()
    for offset in range(1, DEV):
        src = peer_of(me, offset)
        remote(gate_i, gbi.at[src], gs.at[0, offset], gr.at[0, src], me).wait_recv()
        remote(gate_f, gbf.at[src], gs.at[1, offset], gr.at[1, src], me).wait_recv()
    for b in range(DEV):
        rowi[b // 2 : b // 2 + 1, (b % 2) * TOK : (b % 2 + 1) * TOK] = gbi[b, pl.ds(head, 1), :]
        rowf[b // 2 : b // 2 + 1, (b % 2) * TOK : (b % 2 + 1) * TOK] = gbf[b, pl.ds(head, 1), :]
    x = rowf[...]
    log_forget = jnp.minimum(x, 0.0) - jnp.log1p(jnp.exp(-jnp.abs(x)))
    cumul = scan_lanes(log_forget, jnp.add, 0.0)
    lift = rowi[...] - cumul
    lift_max = scan_lanes(lift, jnp.maximum, NEG_FILL)
    decay = cumul[:, CHUNK - 1 : CHUNK]
    peak_in = decay + lift_max[:, CHUNK - 1 : CHUNK]
    peaks = [jnp.full((1, 1), NEG_FILL, jnp.float32)]
    for c in range(8):
        peaks.append(jnp.maximum(decay[c : c + 1] + peaks[-1], peak_in[c : c + 1]))
    first = half == 0
    scales = []
    since = jnp.ones((1, 1), jnp.float32)
    row8 = lax.broadcasted_iota(jnp.int32, (8, CHUNK), 0)
    for c in range(4):
        before = jnp.where(first, peaks[c], peaks[4 + c])
        after = jnp.where(first, peaks[c + 1], peaks[5 + c])
        dec = jnp.where(first, decay[c : c + 1], decay[4 + c : 5 + c])
        lift_c = jnp.where(first, lift[c : c + 1], lift[4 + c : 5 + c])
        top = jnp.maximum(jnp.where(first, lift_max[c : c + 1], lift_max[4 + c : 5 + c]), before)
        weight = jnp.exp(dec + lift_c - after)
        reach = jnp.exp(before - top) * ROOT
        packed = jnp.where(
            row8 == 0, weight, jnp.where(row8 == 1, top, jnp.where(row8 == 2, reach, reach * since))
        )
        tcol[c] = jnp.transpose(packed)
        grow[c] = lift_c
        scales.append(jnp.exp(dec + before - after))
        since = since * scales[-1]

    z_now = jnp.zeros((1, DH), jnp.float32)
    for c in range(4):
        for j in (2 * c, 2 * c + 1):

            @pl.when(j != local)
            def _():
                for part in range(2):
                    piece = kb.at[rows(j), part * 256 : part * 256 + 256]
                    remote(piece, piece, ks.at[part, 0], kr.at[part, j], me).wait_recv()

            @pl.when(j == local)
            def _():
                own[0].wait()

        weighted = kb[c * CHUNK : (c + 1) * CHUNK, :].astype(jnp.float32) * tcol[c][:, 0:1]
        kwt[c] = jnp.transpose(weighted.astype(jnp.bfloat16))
        zst[c] = z_now
        z_now = scales[c] * z_now + jnp.sum(weighted, axis=0, keepdims=True)
    z_out[...] = jnp.broadcast_to(z_now, (8, DH))
    chi[0] = jnp.zeros((DH, DH), jnp.bfloat16)
    clo[0] = jnp.zeros((DH, DH), jnp.bfloat16)

    next_device = 8 + lax.rem(local + 4, 8)
    onward = [remote(z_out, z_in, ss.at[2], sr.at[2], next_device)] + [
        remote(st_out.at[part], st_in.at[part], ss.at[part], sr.at[part], next_device) for part in range(2)
    ]
    for part in range(2):
        cols = slice(part * 256, part * 256 + 256)
        for c in range(4):
            for j in (2 * c, 2 * c + 1):

                @pl.when(j != local)
                def _():
                    piece = vb.at[rows(j), cols]
                    remote(piece, piece, vs.at[part, 0], vr.at[part, j], me).wait_recv()

                if part == 0:

                    @pl.when(j == local)
                    def _():
                        own[1].wait()

            state = jnp.dot(kwt[c], vb[c * CHUNK : (c + 1) * CHUNK, cols], preferred_element_type=jnp.float32)
            if c > 0:
                state += scales[c] * sacc[...]
            high = state.astype(jnp.bfloat16)
            if c < 3:
                sacc[...] = state
                chi[c + 1, :, cols] = high
                clo[c + 1, :, cols] = (state - high.astype(jnp.float32)).astype(jnp.bfloat16)
            else:
                st_out[part] = high

        @pl.when(half == 0)
        def _():
            if part == 0:
                onward[0].start()
            onward[1 + part].start()

    @pl.when(half == 0)
    def _():
        z_in[...] = jnp.zeros((8, DH), jnp.float32)

    @pl.when(half == 1)
    def _():
        for copy in onward:
            copy.wait_recv()

    causal = lax.broadcasted_iota(jnp.int32, (CHUNK, CHUNK), 0) >= lax.broadcasted_iota(
        jnp.int32, (CHUNK, CHUNK), 1
    )
    z_row = lax.broadcasted_iota(jnp.int32, (8, DH), 0)

    @pl.loop(0, 4)
    def _(i):
        c = lax.rem(i + 1 + pair, 4)
        for jj in range(2):
            j = 2 * c + jj

            @pl.when(j != local)
            def _():
                remote(qb.at[rows(j), :], qb.at[rows(j), :], qs.at[0], qr.at[j], me).wait_recv()

            @pl.when(j == local)
            def _():
                own[2].wait()

        part = pl.ds(pl.multiple_of(c * CHUNK, CHUNK), CHUNK)
        query = qb[part, :]
        value = vb[part, :]
        columns = tcol[c]
        top, reach, reach0 = columns[:, 1:2], columns[:, 2:3], columns[:, 3:4]
        weight = jnp.exp(jnp.where(causal, grow[c] - top, NEG_FILL))
        coef = weight * (nt_dot(query, kb[part, :]) * ROOT)
        denom = jnp.sum(coef, axis=1, keepdims=True)
        numer = jnp.dot(coef.astype(jnp.bfloat16), value, preferred_element_type=jnp.float32)
        held = jnp.dot(query, chi[c], preferred_element_type=jnp.float32)
        held += jnp.dot(query, clo[c], preferred_element_type=jnp.float32)
        parts = three_parts(zst[c]) + three_parts(z_in[0:1, :])
        z_all = jnp.zeros((8, DH), jnp.float32)
        for n, piece in enumerate(parts):
            z_all = jnp.where(z_row == n, piece, z_all)
        norm = nt_dot(query, z_all.astype(jnp.bfloat16))
        denom += reach * (norm[:, 0:1] + norm[:, 1:2] + norm[:, 2:3])
        denom += reach0 * (norm[:, 3:4] + norm[:, 4:5] + norm[:, 5:6])
        numer += reach * held

        def finish(total):
            ob[part, :] = (total / jnp.maximum(jnp.abs(denom), 1.0)).astype(jnp.bfloat16)

        @pl.when(half == 0)
        def _():
            finish(numer)

        @pl.when(half == 1)
        def _():
            from_first = jnp.concatenate(
                [jnp.dot(query, st_in[n], preferred_element_type=jnp.float32) for n in range(2)], axis=1
            )
            finish(numer + reach0 * from_first)

        for jj in range(2):
            j = 2 * c + jj

            @pl.when(j != local)
            def _():
                remote(ob.at[rows(j), :], mix.at[head], os.at[j], orr.at[head], base + j).start()

            @pl.when(j == local)
            def _():
                mix[head] = ob[rows(j), :]

    fetched[4].wait()
    for j in range(8):

        @pl.when(j != local)
        def _():
            from_head = lax.rem(j + 4 * half, 8)
            remote(ob.at[rows(j), :], mix.at[from_head], os.at[j], orr.at[from_head], me).wait_recv()

    square = jnp.zeros((TOK, 1), jnp.float32)
    for h in range(HEADS):
        part = mix[h].astype(jnp.float32)
        square += jnp.sum(part * part, axis=1, keepdims=True)
    scale = lax.rsqrt(square * (1.0 / D) + EPSILON)
    square = jnp.zeros((TOK, 1), jnp.float32)
    for h in range(HEADS):
        cols = slice(h * DH, (h + 1) * DH)
        part = residual[:, cols].astype(jnp.float32) + mix[h].astype(jnp.float32) * scale * mix_gain[:, cols]
        rounded = part.astype(jnp.bfloat16)
        upd[:, cols] = rounded
        part = rounded.astype(jnp.float32)
        square += jnp.sum(part * part, axis=1, keepdims=True)
    scale = lax.rsqrt(square * (1.0 / D) + EPSILON)
    for h in range(HEADS):
        cols = slice(h * DH, (h + 1) * DH)
        part = upd[:, cols].astype(jnp.float32)
        acc[:, cols] = part
        normed[:, cols] = (part * scale * ffn_gain[:, cols]).astype(jnp.bfloat16)

    pieces = 4
    depth = CAP // pieces
    for g in range(4):
        for h in range(HEADS):
            cols = slice(h * DH, (h + 1) * DH)
            picked = jnp.dot(picks[g], normed[:, cols], preferred_element_type=jnp.float32)
            disp[g * TOK : (g + 1) * TOK, cols] = picked.astype(jnp.bfloat16)
        for p in range(pieces):
            for n in range(4 * g, 4 * g + 4):
                if n == 0:
                    continue
                piece = pl.ds(n * CAP + p * depth, depth)
                remote(
                    disp.at[piece, :], inbox.at[piece, :], ds.at[n], dr.at[n], peer_of(me, ORDER[n])
                ).start()
    inbox[0:CAP, :] = disp[0:CAP, :]

    def slot_rows(n):
        return pl.ds(n * CAP, CAP)

    for n in range(5, 8):
        fetched[n].wait()

    for g in range(4):
        for n in range(4 * g, 4 * g + 4):
            if n > 0:
                remote(disp.at[slot_rows(n), :], inbox.at[slot_rows(n), :], ds.at[n], dr.at[n], me).wait_recv()
        arrived = inbox[g * TOK : (g + 1) * TOK, :]
        gate = nt_dot(arrived, gate_v[...])
        up = nt_dot(arrived, up_v[...])
        hidden = (gate / (1.0 + jnp.exp(-gate)) * up).astype(jnp.bfloat16)
        for h in range(HEADS):
            cols = slice(h * DH, (h + 1) * DH)
            result[g * TOK : (g + 1) * TOK, cols] = jnp.dot(
                hidden, down_v[:, cols], preferred_element_type=jnp.float32
            ).astype(jnp.bfloat16)
        for p in range(pieces):
            for n in range(4 * g, 4 * g + 4):
                if n == 0:
                    continue
                piece = pl.ds(n * CAP + p * depth, depth)
                back_to = peer_of(me, (4 - ORDER[n] // 4) % 4 * 4 + (4 - ORDER[n] % 4) % 4)
                remote(result.at[piece, :], back.at[piece, :], bs.at[n], br.at[n], back_to).start()
    back[0:CAP, :] = result[0:CAP, :]

    for g in range(4):
        for n in range(4 * g, 4 * g + 4):
            if n > 0:
                remote(result.at[slot_rows(n), :], back.at[slot_rows(n), :], bs.at[n], br.at[n], me).wait_recv()
        for h in range(HEADS):
            cols = slice(h * DH, (h + 1) * DH)
            both = jnp.dot(wmat[g], back[g * TOK : (g + 1) * TOK, cols], preferred_element_type=jnp.float32)
            total = acc[:, cols] + both[0:TOK, :] + both[TOK : 2 * TOK, :]
            if g < 3:
                acc[:, cols] = total
            else:
                out[:, cols] = total.astype(jnp.bfloat16)

    for copy in sent:
        copy.wait_send()

    @pl.when(half == 0)
    def _():
        for copy in onward:
            copy.wait_send()

    for j in range(8):

        @pl.when(j != local)
        def _():
            remote(ob.at[rows(j), :], mix.at[j], os.at[j], orr.at[j], me).wait_send()

    for n in range(1, DEV):
        remote(disp.at[slot_rows(n), :], inbox.at[slot_rows(n), :], ds.at[n], dr.at[n], me).wait_send()
        remote(result.at[slot_rows(n), :], back.at[slot_rows(n), :], bs.at[n], br.at[n], me).wait_send()


def shards(
    queries, key_vectors, value_vectors, residual_in, input_logit, forget_logit, mix_gain, ffn_gain,
    expert_gate, expert_up, expert_down, routes, route_weight,
):
    hbm = pl.BlockSpec(memory_space=pl.ANY)
    dma = pltpu.SemaphoreType.DMA
    vmem = pltpu.VMEM
    bf16, f32 = jnp.bfloat16, jnp.float32
    return pl.pallas_call(
        kernel,
        out_shape=pltpu.VMEM((TOK, D), bf16),
        in_specs=[hbm] * 13,
        out_specs=pl.BlockSpec(memory_space=pltpu.VMEM),
        scratch_shapes=[
            vmem((8 * TOK, DH), bf16),
            vmem((8 * TOK, DH), bf16),
            vmem((8 * TOK, DH), bf16),
            vmem((4, DH, CHUNK), bf16),
            vmem((DEV, HEADS, TOK), f32),
            vmem((DEV, HEADS, TOK), f32),
            vmem((4, DH, DH), bf16),
            vmem((4, DH, DH), bf16),
            vmem((DH, DH // 2), f32),
            vmem((4, 1, DH), f32),
            vmem((8, DH), f32),
            vmem((2, DH, DH // 2), bf16),
            vmem((2, DH, DH // 2), bf16),
            vmem((8, DH), f32),
            vmem((8 * TOK, DH), bf16),
            vmem((HEADS, TOK, DH), bf16),
            vmem((8, CHUNK), f32),
            vmem((8, CHUNK), f32),
            vmem((4, 1, CHUNK), f32),
            vmem((4, CHUNK, 8), f32),
            vmem((TOK, D), bf16),
            vmem((1, D), f32),
            vmem((1, D), f32),
            vmem((2, TOK), jnp.int32),
            vmem((2, TOK), f32),
            vmem((FF, D), bf16),
            vmem((FF, D), bf16),
            vmem((FF, D), bf16),
            vmem((DEV * CAP, D), bf16),
            vmem((DEV * CAP, D), bf16),
            vmem((DEV * CAP, D), bf16),
            vmem((DEV * CAP, D), bf16),
            vmem((TOK, D), bf16),
            vmem((TOK, D), bf16),
            vmem((4, TOK, TOK), bf16),
            vmem((4, 2 * TOK, TOK), bf16),
            vmem((TOK, D), f32),
            dma((5,)),
            dma((8,)),
            dma((2, DEV)),
            dma((2, DEV)),
            dma((2, 7)),
            dma((2, 8)),
            dma((2, 7)),
            dma((2, 8)),
            dma((7,)),
            dma((8,)),
            dma((8,)),
            dma((8,)),
            dma((3,)),
            dma((3,)),
            dma((DEV,)),
            dma((DEV,)),
            dma((DEV,)),
            dma((DEV,)),
        ],
        compiler_params=pltpu.CompilerParams(
            collective_id=0, has_side_effects=True, vmem_limit_bytes=62 << 20
        ),
        name="block",
    )(
        queries,
        key_vectors,
        value_vectors,
        input_logit,
        forget_logit,
        residual_in,
        mix_gain.reshape(1, D),
        ffn_gain.reshape(1, D),
        jnp.transpose(routes),
        jnp.transpose(route_weight),
        jnp.swapaxes(expert_gate[0], 0, 1),
        jnp.swapaxes(expert_up[0], 0, 1),
        expert_down[0],
    )


def solution(mesh):
    return jax.shard_map(
        shards,
        mesh=mesh,
        in_specs=(
            P(("batch", "seq"), None),
            P(("batch", "seq"), None),
            P(("batch", "seq"), None),
            P(("batch", "seq"), None),
            P(None, ("batch", "seq")),
            P(None, ("batch", "seq")),
            P(),
            P(),
            P("seq", None, None),
            P("seq", None, None),
            P("seq", None, None),
            P(("batch", "seq"), None),
            P(("batch", "seq"), None),
        ),
        out_specs=P(("batch", "seq"), None),
        check_vma=False,
    )
```

time: 168 us -> 157 us (0.935)
  Pallas kernels: 165 us -> 156 us
    pallas_call x2 -> x1, Pallas kernels: 165 us -> 156 us  [shards(): pl.pallas_call(kernel, out_shape=pltpu.VMEM((TOK, D), bf16), in_specs=[hb...]
where the time goes in v2:
time: 157 us
  Pallas kernels  156 us (99%)
    pallas_call x1, Pallas kernels, shards(): pl.pallas_call(kernel, out_shape=pltpu.VMEM((TOK, D), bf16), in_specs=[hb...  156 us

profile of v2, /device:TPU:0, one launch (start us, length us, event | category | flops | bytes accessed | tf_op | source)
XLA Modules:
  0.0 157.2 jit_solution(5035371518382734485)
XLA Ops:
  0.0 156.2 %block.1 = bf16[128,4096]{1,0:T(8,128)(2,1)S(1)} custom-call(bf16[128,4096]{1,0:T(8,128)(2,1)} %q_in.1, bf16[128,4096]{1,0:T(8,128)(2,1)} %k_in.1, bf16[128,4096]{1,0:T(8,128)(2,1)} %v_in.1, f32[8,128]{1,0:T(8,128)} %gate_i.1, f32[8,128]{1,0:T(8,128)} %gate_f.1, bf16[128,4096]{1,0:T(8,128)(2,1)} %residual_in.1, f32[1,4096]{1,0:T(1,128)} %bitcast.14, ...), custom_call_target="tpu_custom_call" | custom-call | tf_op jit(solution)/shard_map/block/pallas_call | solution.py:471
  156.2 1.0 copy.15

commit v3 on v2

--- a/solution.py
+++ b/solution.py
@@ -20,7 +20,8 @@
 DEV = 16
 CHUNK = 256
 ROOT = 1.0 / math.sqrt(DH)
-ORDER = (0, 1, 3, 4, 12, 2, 8, 10, 5, 15, 7, 13, 6, 14, 9, 11)
+ORDER = (5, 15, 7, 13, 6, 14, 9, 11, 10, 2, 8, 12, 0, 1, 3, 4)
+SELF = ORDER.index(0)
 NEAR = ((0, 1), (0, 3), (1, 0), (1, 1), (1, 3), (0, 2), (1, 2))
 
 
@@ -50,6 +51,10 @@
     )
 
 
+def settled(ref, semaphore):
+    pltpu.make_async_copy(ref, ref, semaphore).wait()
+
+
 def scan_lanes(x, op, fill):
     lane = lax.broadcasted_iota(jnp.int32, x.shape, 1)
     step = 1
@@ -75,7 +80,7 @@
     qb, kb, vb, kwt, gbi, gbf, chi, clo, sacc, zst, z_in, st_in, st_out, z_out, ob, mix, rowi, rowf, grow, tcol,
     residual, mix_gain, ffn_gain, routes, route_weight,
     gate_v, up_v, down_v, disp, inbox, result, back, upd, normed, picks, wmat, acc,
-    own_sem, w_sem, gs, gr, ks, kr, vs, vr, qs, qr, os, orr, ss, sr, ds, dr, bs, br,
+    own_sem, w_sem, gs, gr, hs, hr, qr, orr, ss, sr, dr, br,
 ):
     me = lax.axis_index("seq")
     half = me // 8
@@ -119,32 +124,27 @@
         copy.start()
     entry_barrier(me)
 
-    sent = []
     for offset in range(1, DEV):
         to = peer_of(me, offset)
         for src, dst, n in ((gate_i, gbi, 0), (gate_f, gbf, 1)):
-            copy = remote(src, dst.at[me], gs.at[n, offset], gr.at[n, me], to)
-            copy.start()
-            sent.append(copy)
+            remote(src, dst.at[me], gs.at[n], gr.at[n], to).start()
 
     def send_part(src, dst, send, recv, lo, width, to):
         to_head = lax.rem(to + 4 * half, 8)
         part = pl.ds(pl.multiple_of(to_head * DH + lo, width), width)
-        copy = remote(src.at[:, part], dst.at[rows(local), lo : lo + width], send, recv, base + to)
-        copy.start()
-        sent.append(copy)
-
-    for src, dst, send, recv in ((k_in, kb, ks, kr), (v_in, vb, vs, vr)):
+        remote(src.at[:, part], dst.at[rows(local), lo : lo + width], send, recv, base + to).start()
+
+    for src, dst, k in ((k_in, kb, 0), (v_in, vb, 1)):
         for part in range(2):
-            for n, (dy, dx) in enumerate(NEAR):
+            for dy, dx in NEAR:
                 to = lax.rem(local // 4 + dy, 2) * 4 + lax.rem(lax.rem(local, 4) + dx, 4)
-                send_part(src, dst, send.at[part, n], recv.at[part, local], part * 256, 256, to)
+                send_part(src, dst, hs.at[k], hr.at[2 * k + part], part * 256, 256, to)
     for n in range(7):
         if n < 6:
             to = 2 * lax.rem(pair + 3 - n // 2, 4) + n % 2
         else:
             to = 2 * pair + 1 - lax.rem(local, 2)
-        send_part(q_in, qb, qs.at[n], qr.at[local], 0, DH, to)
+        send_part(q_in, qb, hs.at[2], qr.at[local], 0, DH, to)
 
     for n in range(4):
         fetched[n].wait()
@@ -186,10 +186,8 @@
 
     for copy in own_gates:
         copy.wait()
-    for offset in range(1, DEV):
-        src = peer_of(me, offset)
-        remote(gate_i, gbi.at[src], gs.at[0, offset], gr.at[0, src], me).wait_recv()
-        remote(gate_f, gbf.at[src], gs.at[1, offset], gr.at[1, src], me).wait_recv()
+    for n, ref in ((0, gbi), (1, gbf)):
+        settled(ref.at[0 : DEV - 1], gr.at[n])
     for b in range(DEV):
         rowi[b // 2 : b // 2 + 1, (b % 2) * TOK : (b % 2 + 1) * TOK] = gbi[b, pl.ds(head, 1), :]
         rowf[b // 2 : b // 2 + 1, (b % 2) * TOK : (b % 2 + 1) * TOK] = gbf[b, pl.ds(head, 1), :]
@@ -224,19 +222,11 @@
         since = since * scales[-1]
 
     z_now = jnp.zeros((1, DH), jnp.float32)
+    own[0].wait()
+    own[1].wait()
+    for part in range(2):
+        settled(kb.at[0 : 7 * TOK, part * 256 : part * 256 + 256], hr.at[part])
     for c in range(4):
-        for j in (2 * c, 2 * c + 1):
-
-            @pl.when(j != local)
-            def _():
-                for part in range(2):
-                    piece = kb.at[rows(j), part * 256 : part * 256 + 256]
-                    remote(piece, piece, ks.at[part, 0], kr.at[part, j], me).wait_recv()
-
-            @pl.when(j == local)
-            def _():
-                own[0].wait()
-
         weighted = kb[c * CHUNK : (c + 1) * CHUNK, :].astype(jnp.float32) * tcol[c][:, 0:1]
         kwt[c] = jnp.transpose(weighted.astype(jnp.bfloat16))
         zst[c] = z_now
@@ -251,20 +241,8 @@
     ]
     for part in range(2):
         cols = slice(part * 256, part * 256 + 256)
+        settled(vb.at[0 : 7 * TOK, cols], hr.at[2 + part])
         for c in range(4):
-            for j in (2 * c, 2 * c + 1):
-
-                @pl.when(j != local)
-                def _():
-                    piece = vb.at[rows(j), cols]
-                    remote(piece, piece, vs.at[part, 0], vr.at[part, j], me).wait_recv()
-
-                if part == 0:
-
-                    @pl.when(j == local)
-                    def _():
-                        own[1].wait()
-
             state = jnp.dot(kwt[c], vb[c * CHUNK : (c + 1) * CHUNK, cols], preferred_element_type=jnp.float32)
             if c > 0:
                 state += scales[c] * sacc[...]
@@ -304,7 +282,7 @@
 
             @pl.when(j != local)
             def _():
-                remote(qb.at[rows(j), :], qb.at[rows(j), :], qs.at[0], qr.at[j], me).wait_recv()
+                settled(qb.at[rows(j), :], qr.at[j])
 
             @pl.when(j == local)
             def _():
@@ -349,20 +327,14 @@
 
             @pl.when(j != local)
             def _():
-                remote(ob.at[rows(j), :], mix.at[head], os.at[j], orr.at[head], base + j).start()
+                remote(ob.at[rows(j), :], mix.at[head], hs.at[3], orr.at[0], base + j).start()
 
             @pl.when(j == local)
             def _():
                 mix[head] = ob[rows(j), :]
 
     fetched[4].wait()
-    for j in range(8):
-
-        @pl.when(j != local)
-        def _():
-            from_head = lax.rem(j + 4 * half, 8)
-            remote(ob.at[rows(j), :], mix.at[from_head], os.at[j], orr.at[from_head], me).wait_recv()
-
+    settled(mix.at[0:7], orr.at[0])
     square = jnp.zeros((TOK, 1), jnp.float32)
     for h in range(HEADS):
         part = mix[h].astype(jnp.float32)
@@ -392,24 +364,22 @@
             disp[g * TOK : (g + 1) * TOK, cols] = picked.astype(jnp.bfloat16)
         for p in range(pieces):
             for n in range(4 * g, 4 * g + 4):
-                if n == 0:
+                if n == SELF:
                     continue
                 piece = pl.ds(n * CAP + p * depth, depth)
                 remote(
-                    disp.at[piece, :], inbox.at[piece, :], ds.at[n], dr.at[n], peer_of(me, ORDER[n])
+                    disp.at[piece, :], inbox.at[piece, :], hs.at[4], dr.at[g], peer_of(me, ORDER[n])
                 ).start()
-    inbox[0:CAP, :] = disp[0:CAP, :]
-
-    def slot_rows(n):
-        return pl.ds(n * CAP, CAP)
+    inbox[SELF * CAP : (SELF + 1) * CAP, :] = disp[SELF * CAP : (SELF + 1) * CAP, :]
+
+    def group_rows(g):
+        return pl.ds(g * TOK, TOK - CAP if SELF // 4 == g else TOK)
 
     for n in range(5, 8):
         fetched[n].wait()
 
     for g in range(4):
-        for n in range(4 * g, 4 * g + 4):
-            if n > 0:
-                remote(disp.at[slot_rows(n), :], inbox.at[slot_rows(n), :], ds.at[n], dr.at[n], me).wait_recv()
+        settled(inbox.at[group_rows(g), :], dr.at[g])
         arrived = inbox[g * TOK : (g + 1) * TOK, :]
         gate = nt_dot(arrived, gate_v[...])
         up = nt_dot(arrived, up_v[...])
@@ -421,17 +391,15 @@
             ).astype(jnp.bfloat16)
         for p in range(pieces):
             for n in range(4 * g, 4 * g + 4):
-                if n == 0:
+                if n == SELF:
                     continue
                 piece = pl.ds(n * CAP + p * depth, depth)
                 back_to = peer_of(me, (4 - ORDER[n] // 4) % 4 * 4 + (4 - ORDER[n] % 4) % 4)
-                remote(result.at[piece, :], back.at[piece, :], bs.at[n], br.at[n], back_to).start()
-    back[0:CAP, :] = result[0:CAP, :]
+                remote(result.at[piece, :], back.at[piece, :], hs.at[5], br.at[g], back_to).start()
+    back[SELF * CAP : (SELF + 1) * CAP, :] = result[SELF * CAP : (SELF + 1) * CAP, :]
 
     for g in range(4):
-        for n in range(4 * g, 4 * g + 4):
-            if n > 0:
-                remote(result.at[slot_rows(n), :], back.at[slot_rows(n), :], bs.at[n], br.at[n], me).wait_recv()
+        settled(back.at[group_rows(g), :], br.at[g])
         for h in range(HEADS):
             cols = slice(h * DH, (h + 1) * DH)
             both = jnp.dot(wmat[g], back[g * TOK : (g + 1) * TOK, cols], preferred_element_type=jnp.float32)
@@ -441,23 +409,17 @@
             else:
                 out[:, cols] = total.astype(jnp.bfloat16)
 
-    for copy in sent:
-        copy.wait_send()
+    for n, ref in ((0, gbi), (1, gbf)):
+        settled(ref.at[0 : DEV - 1], gs.at[n])
+    for n, ref in ((0, kb), (1, vb), (2, qb), (3, ob)):
+        settled(ref.at[0 : 7 * TOK, :], hs.at[n])
+    for n, ref in ((4, disp), (5, result)):
+        settled(ref.at[0 : (DEV - 1) * CAP, :], hs.at[n])
 
     @pl.when(half == 0)
     def _():
         for copy in onward:
             copy.wait_send()
-
-    for j in range(8):
-
-        @pl.when(j != local)
-        def _():
-            remote(ob.at[rows(j), :], mix.at[j], os.at[j], orr.at[j], me).wait_send()
-
-    for n in range(1, DEV):
-        remote(disp.at[slot_rows(n), :], inbox.at[slot_rows(n), :], ds.at[n], dr.at[n], me).wait_send()
-        remote(result.at[slot_rows(n), :], back.at[slot_rows(n), :], bs.at[n], br.at[n], me).wait_send()
 
 
 def shards(
@@ -513,22 +475,16 @@
             vmem((TOK, D), f32),
             dma((5,)),
             dma((8,)),
-            dma((2, DEV)),
-            dma((2, DEV)),
-            dma((2, 7)),
-            dma((2, 8)),
-            dma((2, 7)),
-            dma((2, 8)),
-            dma((7,)),
+            dma((2,)),
+            dma((2,)),
+            dma((6,)),
+            dma((4,)),
             dma((8,)),
-            dma((8,)),
-            dma((8,)),
+            dma((1,)),
             dma((3,)),
             dma((3,)),
-            dma((DEV,)),
-            dma((DEV,)),
-            dma((DEV,)),
-            dma((DEV,)),
+            dma((4,)),
+            dma((4,)),
         ],
         compiler_params=pltpu.CompilerParams(
             collective_id=0, has_side_effects=True, vmem_limit_bytes=62 << 20

time: 157 us -> 153 us (0.975)
  Pallas kernels: 156 us -> 152 us
    pallas_call x1, Pallas kernels: 156 us -> 152 us  [shards(): pl.pallas_call(kernel, out_shape=pltpu.VMEM((TOK, D), bf16), in_specs=[hb...]
where the time goes in v3:
time: 153 us
  Pallas kernels  152 us (99%)
    pallas_call x1, Pallas kernels, shards(): pl.pallas_call(kernel, out_shape=pltpu.VMEM((TOK, D), bf16), in_specs=[hb...  152 us

profile of v3, /device:TPU:0, one launch (start us, length us, event | category | flops | bytes accessed | tf_op | source)
XLA Modules:
  0.0 152.8 jit_solution(6240942737248439091)
XLA Ops:
  0.0 151.9 %block.1 = bf16[128,4096]{1,0:T(8,128)(2,1)S(1)} custom-call(bf16[128,4096]{1,0:T(8,128)(2,1)} %q_in.1, bf16[128,4096]{1,0:T(8,128)(2,1)} %k_in.1, bf16[128,4096]{1,0:T(8,128)(2,1)} %v_in.1, f32[8,128]{1,0:T(8,128)} %gate_i.1, f32[8,128]{1,0:T(8,128)} %gate_f.1, bf16[128,4096]{1,0:T(8,128)(2,1)} %residual_in.1, f32[1,4096]{1,0:T(1,128)} %bitcast.14, ...), custom_call_target="tpu_custom_call" | custom-call | tf_op jit(solution)/shard_map/block/pallas_call | solution.py:433
  151.9 1.0 copy.15

commit v4 on v3

--- a/solution.py
+++ b/solution.py
@@ -22,6 +22,7 @@
 ROOT = 1.0 / math.sqrt(DH)
 ORDER = (5, 15, 7, 13, 6, 14, 9, 11, 10, 2, 8, 12, 0, 1, 3, 4)
 SELF = ORDER.index(0)
+WIDE = D // 2
 NEAR = ((0, 1), (0, 3), (1, 0), (1, 1), (1, 3), (0, 2), (1, 2))
 
 
@@ -79,8 +80,8 @@
     q_in, k_in, v_in, gate_i, gate_f, residual_in, gain_m, gain_f, routes_in, share_in, w_gate, w_up, w_down, out,
     qb, kb, vb, kwt, gbi, gbf, chi, clo, sacc, zst, z_in, st_in, st_out, z_out, ob, mix, rowi, rowf, grow, tcol,
     residual, mix_gain, ffn_gain, routes, route_weight,
-    gate_v, up_v, down_v, disp, inbox, result, back, upd, normed, picks, wmat, acc,
-    own_sem, w_sem, gs, gr, hs, hr, qr, orr, ss, sr, dr, br,
+    gate_v, up_v, down_v, disp, inbox, result, back, upd, normed, picks, wmat, acc, rb, mates,
+    own_sem, w_sem, gs, gr, hs, hr, qr, orr, ss, sr, dr, br, fr, ar, sr2,
 ):
     me = lax.axis_index("seq")
     half = me // 8
@@ -129,6 +130,13 @@
         for src, dst, n in ((gate_i, gbi, 0), (gate_f, gbf, 1)):
             remote(src, dst.at[me], gs.at[n], gr.at[n], to).start()
 
+    def along(axis, d):
+        return peer_of(me, d if axis == 0 else 4 * d)
+
+    for axis in range(2):
+        for d in range(1, 4):
+            remote(routes_in, mates.at[me], gs.at[2], gr.at[2], along(axis, d)).start()
+
     def send_part(src, dst, send, recv, lo, width, to):
         to_head = lax.rem(to + 4 * half, 8)
         part = pl.ds(pl.multiple_of(to_head * DH + lo, width), width)
@@ -180,9 +188,24 @@
     for g in range(4):
         wmat[g, 0:TOK, :] = high[:, g * TOK : (g + 1) * TOK]
         wmat[g, TOK : 2 * TOK, :] = low[:, g * TOK : (g + 1) * TOK]
-        target = lax.broadcasted_iota(jnp.int32, (TOK, TOK), 0) + g * TOK
-        pick = jnp.where((target == slot0.astype(jnp.int32)) | (target == slot1.astype(jnp.int32)), 1.0, 0.0)
-        picks[g] = pick.astype(jnp.bfloat16)
+
+    settled(mates.at[0:6], gr.at[2])
+    target = lax.broadcasted_iota(jnp.int32, (TOK, TOK), 0).astype(jnp.float32)
+    upper = jnp.where(earlier, 1.0, 0.0).astype(jnp.bfloat16)
+    for axis in range(2):
+        owner = jnp.full((DEV, TOK), -1, jnp.int32)
+        for t in range(4):
+            owner = jnp.where(row16 == t, along(1 - axis, t), owner)
+        for d in range(4):
+            named = routes[...] if d == 0 else mates[along(axis, d)]
+            hit0 = named[0:1, :] == owner
+            hit1 = named[1:2, :] == owner
+            match = jnp.where(hit0 | hit1, 1.0, 0.0).astype(jnp.bfloat16)
+            slot = jnp.dot(match, upper, preferred_element_type=jnp.float32) + (row16 * CAP + 1).astype(jnp.float32)
+            slot0 = jnp.sum(jnp.where(hit0, slot, 0.0), axis=0, keepdims=True) - 1.0
+            slot1 = jnp.sum(jnp.where(hit1, slot, 0.0), axis=0, keepdims=True) - 1.0
+            pick = jnp.where((target == slot0) | (target == slot1), 1.0, 0.0)
+            picks[axis, d] = pick.astype(jnp.bfloat16)
 
     for copy in own_gates:
         copy.wait()
@@ -357,29 +380,79 @@
 
     pieces = 4
     depth = CAP // pieces
-    for g in range(4):
-        for h in range(HEADS):
-            cols = slice(h * DH, (h + 1) * DH)
-            picked = jnp.dot(picks[g], normed[:, cols], preferred_element_type=jnp.float32)
-            disp[g * TOK : (g + 1) * TOK, cols] = picked.astype(jnp.bfloat16)
-        for p in range(pieces):
-            for n in range(4 * g, 4 * g + 4):
-                if n == SELF:
-                    continue
-                piece = pl.ds(n * CAP + p * depth, depth)
+
+    def quarter(p):
+        return slice(p * 512, p * 512 + 512)
+
+    def gather_sems(axis, way, p):
+        if p // 2 == way:
+            return fr.at[axis, way, p % 2]
+        return ar.at[axis, way]
+
+    for k in range(4):
+        for axis in range(2):
+            for way in range(2):
+                p = (k + 2 * way) % 4
                 remote(
-                    disp.at[piece, :], inbox.at[piece, :], hs.at[4], dr.at[g], peer_of(me, ORDER[n])
+                    normed.at[:, axis * WIDE + p * 512 : axis * WIDE + p * 512 + 512],
+                    rb.at[axis, 2 - 2 * way, :, quarter(p)],
+                    hs.at[6],
+                    gather_sems(axis, way, p),
+                    along(axis, 1 + 2 * way),
                 ).start()
-    inbox[SELF * CAP : (SELF + 1) * CAP, :] = disp[SELF * CAP : (SELF + 1) * CAP, :]
+
+    def block_of(axis, d, t):
+        back_d = (4 - d) % 4
+        return ORDER.index(t * 4 + back_d if axis == 0 else back_d * 4 + t)
+
+    def pass_on(axis, d):
+        for p in range(4):
+            cols = slice(axis * WIDE + p * 512, axis * WIDE + p * 512 + 512)
+            rows_here = normed[:, cols] if d == 0 else rb[axis, d - 1, :, quarter(p)]
+            picked = jnp.dot(picks[axis, d], rows_here, preferred_element_type=jnp.float32)
+            disp[d * TOK : (d + 1) * TOK, cols] = picked.astype(jnp.bfloat16)
+        cols = slice(axis * WIDE, (axis + 1) * WIDE)
+        for part in range(2):
+            for t in (1, 3, 2):
+                n = block_of(axis, d, t)
+                remote(
+                    disp.at[pl.ds(d * TOK + t * CAP + part * 16, 16), cols],
+                    inbox.at[pl.ds(n * CAP + part * 16, 16), cols],
+                    hs.at[4],
+                    dr.at[n // 4],
+                    along(1 - axis, t),
+                ).start()
+        n = block_of(axis, d, 0)
+        inbox[n * CAP : (n + 1) * CAP, cols] = disp[d * TOK : d * TOK + CAP, cols]
+
+    pass_on(0, 0)
+    pass_on(1, 0)
+    for k in range(2):
+        for axis in range(2):
+            for way in range(2):
+                p = 2 * way + k
+                came = rb.at[axis, 2 - 2 * way, :, quarter(p)]
+                settled(came, fr.at[axis, way, k])
+                remote(came, rb.at[axis, 1, :, quarter(p)], hs.at[6], sr2.at[axis], along(axis, 1 + 2 * way)).start()
+    for axis in range(2):
+        for way in range(2):
+            settled(rb.at[axis, 2 - 2 * way, :, 0:1024], ar.at[axis, way])
+            pass_on(axis, 3 - 2 * way)
+    for axis in range(2):
+        settled(rb.at[axis, 1], sr2.at[axis])
+        pass_on(axis, 2)
 
     def group_rows(g):
         return pl.ds(g * TOK, TOK - CAP if SELF // 4 == g else TOK)
 
+    def halves_from_others(g):
+        return sum((o // 4 != 0) + (o % 4 != 0) for o in ORDER[4 * g : 4 * g + 4])
+
     for n in range(5, 8):
         fetched[n].wait()
 
     for g in range(4):
-        settled(inbox.at[group_rows(g), :], dr.at[g])
+        settled(inbox.at[0 : CAP * halves_from_others(g), 0:WIDE], dr.at[g])
         arrived = inbox[g * TOK : (g + 1) * TOK, :]
         gate = nt_dot(arrived, gate_v[...])
         up = nt_dot(arrived, up_v[...])
@@ -413,8 +486,10 @@
         settled(ref.at[0 : DEV - 1], gs.at[n])
     for n, ref in ((0, kb), (1, vb), (2, qb), (3, ob)):
         settled(ref.at[0 : 7 * TOK, :], hs.at[n])
-    for n, ref in ((4, disp), (5, result)):
-        settled(ref.at[0 : (DEV - 1) * CAP, :], hs.at[n])
+    settled(mates.at[0:6], gs.at[2])
+    settled(disp.at[0 : 12 * CAP, :], hs.at[4])
+    settled(result.at[0 : (DEV - 1) * CAP, :], hs.at[5])
+    settled(rb, hs.at[6])
 
     @pl.when(half == 0)
     def _():
@@ -470,14 +545,16 @@
             vmem((DEV * CAP, D), bf16),
             vmem((TOK, D), bf16),
             vmem((TOK, D), bf16),
-            vmem((4, TOK, TOK), bf16),
+            vmem((2, 4, TOK, TOK), bf16),
             vmem((4, 2 * TOK, TOK), bf16),
             vmem((TOK, D), f32),
+            vmem((2, 3, TOK, WIDE), bf16),
+            vmem((DEV, 2, TOK), jnp.int32),
             dma((5,)),
             dma((8,)),
-            dma((2,)),
-            dma((2,)),
-            dma((6,)),
+            dma((3,)),
+            dma((3,)),
+            dma((7,)),
             dma((4,)),
             dma((8,)),
             dma((1,)),
@@ -485,6 +562,9 @@
             dma((3,)),
             dma((4,)),
             dma((4,)),
+            dma((2, 2, 2)),
+            dma((2, 2)),
+            dma((2,)),
         ],
         compiler_params=pltpu.CompilerParams(
             collective_id=0, has_side_effects=True, vmem_limit_bytes=62 << 20

time: 153 us -> 148 us (0.967)
  Pallas kernels: 152 us -> 146 us
    pallas_call x1, Pallas kernels: 152 us -> 146 us  [shards(): pl.pallas_call(kernel, out_shape=pltpu.VMEM((TOK, D), bf16), in_specs=[hb...]
where the time goes in v4:
time: 148 us; the launch traced here: 147 us
  Pallas kernels  146 us (99%)
    pallas_call x1, Pallas kernels, shards(): pl.pallas_call(kernel, out_shape=pltpu.VMEM((TOK, D), bf16), in_specs=[hb...  146 us

profile of v4, /device:TPU:0, one launch (start us, length us, event | category | flops | bytes accessed | tf_op | source)
XLA Modules:
  0.0 147.4 jit_solution(15063281788889076632)
XLA Ops:
  0.0 146.4 %block.1 = bf16[128,4096]{1,0:T(8,128)(2,1)S(1)} custom-call(bf16[128,4096]{1,0:T(8,128)(2,1)} %q_in.1, bf16[128,4096]{1,0:T(8,128)(2,1)} %k_in.1, bf16[128,4096]{1,0:T(8,128)(2,1)} %v_in.1, f32[8,128]{1,0:T(8,128)} %gate_i.1, f32[8,128]{1,0:T(8,128)} %gate_f.1, bf16[128,4096]{1,0:T(8,128)(2,1)} %residual_in.1, f32[1,4096]{1,0:T(1,128)} %bitcast.14, ...), custom_call_target="tpu_custom_call" | custom-call | tf_op jit(solution)/shard_map/block/pallas_call | solution.py:508
  146.4 1.0 copy.15

commit v5 on v4

--- a/solution.py
+++ b/solution.py
@@ -378,9 +378,6 @@
         acc[:, cols] = part
         normed[:, cols] = (part * scale * ffn_gain[:, cols]).astype(jnp.bfloat16)
 
-    pieces = 4
-    depth = CAP // pieces
-
     def quarter(p):
         return slice(p * 512, p * 512 + 512)
 
@@ -457,27 +454,29 @@
         gate = nt_dot(arrived, gate_v[...])
         up = nt_dot(arrived, up_v[...])
         hidden = (gate / (1.0 + jnp.exp(-gate)) * up).astype(jnp.bfloat16)
-        for h in range(HEADS):
-            cols = slice(h * DH, (h + 1) * DH)
-            result[g * TOK : (g + 1) * TOK, cols] = jnp.dot(
-                hidden, down_v[:, cols], preferred_element_type=jnp.float32
-            ).astype(jnp.bfloat16)
-        for p in range(pieces):
-            for n in range(4 * g, 4 * g + 4):
-                if n == SELF:
-                    continue
-                piece = pl.ds(n * CAP + p * depth, depth)
-                back_to = peer_of(me, (4 - ORDER[n] // 4) % 4 * 4 + (4 - ORDER[n] % 4) % 4)
-                remote(result.at[piece, :], back.at[piece, :], hs.at[5], br.at[g], back_to).start()
+        for side in range(2):
+            for h in range(4 * side, 4 * side + 4):
+                cols = slice(h * DH, (h + 1) * DH)
+                result[g * TOK : (g + 1) * TOK, cols] = jnp.dot(
+                    hidden, down_v[:, cols], preferred_element_type=jnp.float32
+                ).astype(jnp.bfloat16)
+            cols = slice(side * WIDE, (side + 1) * WIDE)
+            for part in range(2):
+                for n in range(4 * g, 4 * g + 4):
+                    if n == SELF:
+                        continue
+                    piece = pl.ds(n * CAP + part * 16, 16)
+                    back_to = peer_of(me, (4 - ORDER[n] // 4) % 4 * 4 + (4 - ORDER[n] % 4) % 4)
+                    remote(result.at[piece, cols], back.at[piece, cols], hs.at[5], br.at[g], back_to).start()
     back[SELF * CAP : (SELF + 1) * CAP, :] = result[SELF * CAP : (SELF + 1) * CAP, :]
 
-    for g in range(4):
+    for turn, g in enumerate(range(4)):
         settled(back.at[group_rows(g), :], br.at[g])
         for h in range(HEADS):
             cols = slice(h * DH, (h + 1) * DH)
             both = jnp.dot(wmat[g], back[g * TOK : (g + 1) * TOK, cols], preferred_element_type=jnp.float32)
             total = acc[:, cols] + both[0:TOK, :] + both[TOK : 2 * TOK, :]
-            if g < 3:
+            if turn < 3:
                 acc[:, cols] = total
             else:
                 out[:, cols] = total.astype(jnp.bfloat16)

time: 148 us -> 147 us (level)
  no operation moved by 1% of the time
where the time goes in v5:
time: 147 us
  Pallas kernels  146 us (99%)
    pallas_call x1, Pallas kernels, shards(): pl.pallas_call(kernel, out_shape=pltpu.VMEM((TOK, D), bf16), in_specs=[hb...  146 us

profile of v5, /device:TPU:0, one launch (start us, length us, event | category | flops | bytes accessed | tf_op | source)
XLA Modules:
  0.0 147.4 jit_solution(12129225524802501204)
XLA Ops:
  0.0 146.4 %block.1 = bf16[128,4096]{1,0:T(8,128)(2,1)S(1)} custom-call(bf16[128,4096]{1,0:T(8,128)(2,1)} %q_in.1, bf16[128,4096]{1,0:T(8,128)(2,1)} %k_in.1, bf16[128,4096]{1,0:T(8,128)(2,1)} %v_in.1, f32[8,128]{1,0:T(8,128)} %gate_i.1, f32[8,128]{1,0:T(8,128)} %gate_f.1, bf16[128,4096]{1,0:T(8,128)(2,1)} %residual_in.1, f32[1,4096]{1,0:T(1,128)} %bitcast.14, ...), custom_call_target="tpu_custom_call" | custom-call | tf_op jit(solution)/shard_map/block/pallas_call | solution.py:507
  146.4 1.0 copy.15
